TPU v7x, 512 devices: a whole 4x8x8 slice. The times are simulated.
512 devices in a mesh: rep: 256 (over y_lo, x, z, core), slab: 2 (over y_hi).
Axes of the slice: x: 4, y: 8 (y_hi: 2, y_lo: 4; y = y_hi * 4 + y_lo), z: 8, core: 2. Of those that a mesh axis runs over, the one named last changes fastest.
Arguments:
- weights: bfloat16 [256, 256, 3072], P('rep', 'slab'), may hold values from -6 to 6
- perms: int32 [256, 8, 256], P('rep'), may hold values from 0 to 255, each once within a row
Outputs:
- merged: bfloat16 [256, 256, 3072], P('rep', 'slab')
Inputs may be any that keep to these rules, and one draw needn't show every extreme that they name: `perms`: each row of 256 entries names every neuron of the window once.
All inputs are finite; a program needn't handle non-finite values.
Results may differ from a plain program's by a relative error of at most 0.012.
Values may be sent and summed in bfloat16 or wider, within the bound.
A program may use at most 64 MiB of HBM per device.

v0:
```python
import math

import jax
import jax.numpy as jnp
from jax import lax
from jax.sharding import PartitionSpec as P

D = 3072
ROUNDS = 8


def from_partner(x, axis, stride):
    return lax.ppermute(x, axis, [(i, i ^ 1 << stride) for i in range(lax.axis_size(axis))])


def over_pieces(x, axis):
    return lax.all_gather(x, axis).sum(0)


def finish_round(own, partner, perm_rows, cost):
    squared = cost * cost
    fourth = squared * squared
    soft_plan = fourth / (1.0 + jnp.sum(fourth, axis=1, keepdims=True))
    columns = jnp.arange(partner.shape[0], dtype=jnp.int32)
    onehot = (perm_rows[:, None] == columns[None, :]).astype(jnp.float32)
    mixing = (onehot + soft_plan).astype(jnp.bfloat16)
    aligned = 0.5 * jnp.dot(mixing, partner, preferred_element_type=jnp.float32)
    return ((own.astype(jnp.float32) + aligned) * (1.0 / math.sqrt(2.0))).astype(jnp.bfloat16)


def local(weights, perms):
    bit_count = lax.axis_size("rep").bit_length() - 1
    current = weights[0]
    perm_plan = perms[0]
    feature_part = lax.all_to_all(current, "slab", split_axis=1, concat_axis=0, tiled=True)
    for round_idx in range(ROUNDS):
        partner = from_partner(feature_part, "rep", round_idx % bit_count)
        partial_value = jnp.dot(feature_part, partner.T, preferred_element_type=jnp.float32)
        cost = over_pieces(partial_value, "slab") * (1.0 / math.sqrt(D))
        feature_part = finish_round(feature_part, partner, perm_plan[round_idx], cost)
    result = lax.all_to_all(feature_part, "slab", split_axis=0, concat_axis=1, tiled=True)
    return result[None]


def solution(mesh):
    placed = (P("rep", "slab", None), P("rep", None, None))
    return jax.shard_map(
        local, mesh=mesh, in_specs=placed, out_specs=P("rep", "slab", None), check_vma=False
    )
```

profile of v0, /device:TPU:57, one launch (start us, length us, event | category | flops | bytes accessed | tf_op | source)
XLA Modules:
  0.0 361.0 jit_solution(1746409043546388036)
XLA Ops:
  0.0 2.6 all_to_all.26
  2.7 15.5 %all_to_all.35 = bf16[128,2,1536]{2,0,1:T(8,128)(2,1)S(1)} all-to-all(bf16[128,2,1536]{2,0,1:T(8,128)(2,1)S(1)} %copy.5), channel_id=1, replica_groups=mesh['rep'=256,'slab'=2] {'slab'}, dimensions={1} | all-to-all | bytes 1572864 | tf_op jit(solution)/shard_map/all_to_all | solution.py:35
  18.2 3.5 collective-permute-start
  21.7 1.9 collective-permute-done
  24.0 20.2 %all-gather = f32[512,256]{1,0:T(8,128)S(1)} all-gather(f32[256,256]{1,0:T(8,128)S(1)} %fusion.65), channel_id=2, replica_groups=mesh['rep'=256,'slab'=2] {'slab'}, dimensions={0}, use_global_device_ids=true | all-gather | bytes 786432 | tf_op jit(solution)/shard_map/all_gather | solution.py:17
  44.3 0.5 fusion.16
  44.8 4.0 %collective-permute-start.1 = (bf16[256,1536]{1,0:T(8,128)(2,1)S(1)}, bf16[256,1536]{1,0:T(8,128)(2,1)S(1)}, u32[]{:S(2)}, u32[]{:S(2)}) collective-permute-start(bf16[256,1536]{1,0:T(8,128)(2,1)S(1)} %fusion.16), channel_id=1, source_target_pairs={{0,4},{2,6},{4,0},{6,2},{8,12},{10,14},{12,8},{14,10},{16,20},{18,... | collective-permute-start | bytes 2359304 | tf_op jit(solution)/shard_map/ppermute | solution.py:13
  48.8 12.1 %collective-permute-done.1 = bf16[256,1536]{1,0:T(8,128)(2,1)S(1)} collective-permute-done((bf16[256,1536]{1,0:T(8,128)(2,1)S(1)}, bf16[256,1536]{1,0:T(8,128)(2,1)S(1)}, u32[]{:S(2)}, u32[]{:S(2)}) %collective-permute-start.1) | collective-permute-done | bytes 786464 | tf_op jit(solution)/shard_map/ppermute | solution.py:13
  61.2 9.8 %all-gather.1 = f32[512,256]{1,0:T(8,128)S(1)} all-gather(f32[256,256]{1,0:T(8,128)S(1)} %fusion.66), channel_id=3, replica_groups=mesh['rep'=256,'slab'=2] {'slab'}, dimensions={0}, use_global_device_ids=true | all-gather | bytes 786432 | tf_op jit(solution)/shard_map/all_gather | solution.py:17
  71.7 5.8 %collective-permute-start.2 = (bf16[256,1536]{1,0:T(8,128)(2,1)S(1)}, bf16[256,1536]{1,0:T(8,128)(2,1)S(1)}, u32[]{:S(2)}, u32[]{:S(2)}) collective-permute-start(bf16[256,1536]{1,0:T(8,128)(2,1)S(1)} %fusion.17), channel_id=1, source_target_pairs={{0,8},{2,10},{4,12},{6,14},{8,0},{10,2},{12,4},{14,6},{16,24},{18,... | collective-permute-start | bytes 2359304 | tf_op jit(solution)/shard_map/ppermute | solution.py:13
  77.5 34.0 %collective-permute-done.2 = bf16[256,1536]{1,0:T(8,128)(2,1)S(1)} collective-permute-done((bf16[256,1536]{1,0:T(8,128)(2,1)S(1)}, bf16[256,1536]{1,0:T(8,128)(2,1)S(1)}, u32[]{:S(2)}, u32[]{:S(2)}) %collective-permute-start.2) | collective-permute-done | bytes 786464 | tf_op jit(solution)/shard_map/ppermute | solution.py:13
  111.9 11.0 %all-gather.2 = f32[512,256]{1,0:T(8,128)S(1)} all-gather(f32[256,256]{1,0:T(8,128)S(1)} %fusion.67), channel_id=4, replica_groups=mesh['rep'=256,'slab'=2] {'slab'}, dimensions={0}, use_global_device_ids=true | all-gather | bytes 786432 | tf_op jit(solution)/shard_map/all_gather | solution.py:17
  123.5 8.1 %collective-permute-start.3 = (bf16[256,1536]{1,0:T(8,128)(2,1)S(1)}, bf16[256,1536]{1,0:T(8,128)(2,1)S(1)}, u32[]{:S(2)}, u32[]{:S(2)}) collective-permute-start(bf16[256,1536]{1,0:T(8,128)(2,1)S(1)} %fusion.18), channel_id=1, source_target_pairs={{0,16},{2,18},{4,20},{6,22},{8,24},{10,26},{12,28},{14,30},{16,0},... | collective-permute-start | bytes 2359304 | tf_op jit(solution)/shard_map/ppermute | solution.py:13
  131.6 32.9 %collective-permute-done.3 = bf16[256,1536]{1,0:T(8,128)(2,1)S(1)} collective-permute-done((bf16[256,1536]{1,0:T(8,128)(2,1)S(1)}, bf16[256,1536]{1,0:T(8,128)(2,1)S(1)}, u32[]{:S(2)}, u32[]{:S(2)}) %collective-permute-start.3) | collective-permute-done | bytes 786464 | tf_op jit(solution)/shard_map/ppermute | solution.py:13
  164.9 9.8 %all-gather.3 = f32[512,256]{1,0:T(8,128)S(1)} all-gather(f32[256,256]{1,0:T(8,128)S(1)} %fusion.68), channel_id=5, replica_groups=mesh['rep'=256,'slab'=2] {'slab'}, dimensions={0}, use_global_device_ids=true | all-gather | bytes 786432 | tf_op jit(solution)/shard_map/all_gather | solution.py:17
  174.8 0.5 fusion.19
  175.3 3.1 collective-permute-start.4
  178.4 13.9 %collective-permute-done.4 = bf16[256,1536]{1,0:T(8,128)(2,1)S(1)} collective-permute-done((bf16[256,1536]{1,0:T(8,128)(2,1)S(1)}, bf16[256,1536]{1,0:T(8,128)(2,1)S(1)}, u32[]{:S(2)}, u32[]{:S(2)}) %collective-permute-start.4) | collective-permute-done | bytes 786464 | tf_op jit(solution)/shard_map/ppermute | solution.py:13
  192.7 9.8 %all-gather.4 = f32[512,256]{1,0:T(8,128)S(1)} all-gather(f32[256,256]{1,0:T(8,128)S(1)} %fusion.69), channel_id=6, replica_groups=mesh['rep'=256,'slab'=2] {'slab'}, dimensions={0}, use_global_device_ids=true | all-gather | bytes 786432 | tf_op jit(solution)/shard_map/all_gather | solution.py:17
  203.2 4.8 %collective-permute-start.5 = (bf16[256,1536]{1,0:T(8,128)(2,1)S(1)}, bf16[256,1536]{1,0:T(8,128)(2,1)S(1)}, u32[]{:S(2)}, u32[]{:S(2)}) collective-permute-start(bf16[256,1536]{1,0:T(8,128)(2,1)S(1)} %fusion.20), channel_id=1, source_target_pairs={{0,64},{2,66},{4,68},{6,70},{8,72},{10,74},{12,76},{14,78},{16,80}... | collective-permute-start | bytes 2359304 | tf_op jit(solution)/shard_map/ppermute | solution.py:13
  208.0 11.7 %collective-permute-done.5 = bf16[256,1536]{1,0:T(8,128)(2,1)S(1)} collective-permute-done((bf16[256,1536]{1,0:T(8,128)(2,1)S(1)}, bf16[256,1536]{1,0:T(8,128)(2,1)S(1)}, u32[]{:S(2)}, u32[]{:S(2)}) %collective-permute-start.5) | collective-permute-done | bytes 786464 | tf_op jit(solution)/shard_map/ppermute | solution.py:13
  220.1 9.8 %all-gather.5 = f32[512,256]{1,0:T(8,128)S(1)} all-gather(f32[256,256]{1,0:T(8,128)S(1)} %fusion.70), channel_id=7, replica_groups=mesh['rep'=256,'slab'=2] {'slab'}, dimensions={0}, use_global_device_ids=true | all-gather | bytes 786432 | tf_op jit(solution)/shard_map/all_gather | solution.py:17
  230.5 18.9 %collective-permute-start.6 = (bf16[256,1536]{1,0:T(8,128)(2,1)S(1)}, bf16[256,1536]{1,0:T(8,128)(2,1)S(1)}, u32[]{:S(2)}, u32[]{:S(2)}) collective-permute-start(bf16[256,1536]{1,0:T(8,128)(2,1)S(1)} %fusion.21), channel_id=1, source_target_pairs={{0,128},{2,130},{4,132},{6,134},{8,136},{10,138},{12,140},{14,142}... | collective-permute-start | bytes 2359304 | tf_op jit(solution)/shard_map/ppermute | solution.py:13
  249.5 13.2 %collective-permute-done.6 = bf16[256,1536]{1,0:T(8,128)(2,1)S(1)} collective-permute-done((bf16[256,1536]{1,0:T(8,128)(2,1)S(1)}, bf16[256,1536]{1,0:T(8,128)(2,1)S(1)}, u32[]{:S(2)}, u32[]{:S(2)}) %collective-permute-start.6) | collective-permute-done | bytes 786464 | tf_op jit(solution)/shard_map/ppermute | solution.py:13
  263.1 14.4 %all-gather.6 = f32[512,256]{1,0:T(8,128)S(1)} all-gather(f32[256,256]{1,0:T(8,128)S(1)} %fusion.71), channel_id=8, replica_groups=mesh['rep'=256,'slab'=2] {'slab'}, dimensions={0}, use_global_device_ids=true | all-gather | bytes 786432 | tf_op jit(solution)/shard_map/all_gather | solution.py:17
  278.1 1.9 collective-permute-start.7
  280.0 40.1 %collective-permute-done.7 = bf16[256,1536]{1,0:T(8,128)(2,1)S(1)} collective-permute-done((bf16[256,1536]{1,0:T(8,128)(2,1)S(1)}, bf16[256,1536]{1,0:T(8,128)(2,1)S(1)}, u32[]{:S(2)}, u32[]{:S(2)}) %collective-permute-start.7) | collective-permute-done | bytes 786464 | tf_op jit(solution)/shard_map/ppermute | solution.py:13
  320.6 14.7 %all-gather.7 = f32[512,256]{1,0:T(8,128)S(1)} all-gather(f32[256,256]{1,0:T(8,128)S(1)} %fusion.72), channel_id=9, replica_groups=mesh['rep'=256,'slab'=2] {'slab'}, dimensions={0}, use_global_device_ids=true | all-gather | bytes 786432 | tf_op jit(solution)/shard_map/all_gather | solution.py:17
  335.4 0.5 fusion.23
  335.9 22.8 %all_to_all.36 = bf16[2,128,1536]{2,1,0:T(8,128)(2,1)S(1)} all-to-all(bf16[2,128,1536]{2,1,0:T(8,128)(2,1)S(1)} %bitcast.57), channel_id=1, replica_groups=mesh['rep'=256,'slab'=2] {'slab'}, dimensions={0} | all-to-all | bytes 1572864 | tf_op jit(solution)/shard_map/all_to_all | solution.py:41
  358.7 0.8 copy.6
  359.5 1.5 broadcast_in_dim.2
  (41 shorter events, 6.8 us)
Async XLA Ops:
  2.7 19.0 %copy-start = (s32[1,8,256]{2,1,0:T(8,128)S(1)}, s32[1,8,256]{2,1,0:T(8,128)}, u32[]{:S(2)}) copy-start(s32[1,8,256]{2,1,0:T(8,128)} %param.3) | copy-start | bytes 24580
  18.2 5.4 %collective-permute-start = (bf16[256,1536]{1,0:T(8,128)(2,1)S(1)}, bf16[256,1536]{1,0:T(8,128)(2,1)S(1)}, u32[]{:S(2)}, u32[]{:S(2)}) collective-permute-start(bf16[256,1536]{1,0:T(8,128)(2,1)S(1)} %bitcast.45), channel_id=1, source_target_pairs={{0,2},{2,0},{4,6},{6,4},{8,10},{10,8},{12,14},{14,12},{16,18},{18,... | collective-permute-start | bytes 2359304 | tf_op jit(solution)/shard_map/ppermute | solution.py:13
  44.8 16.1 %collective-permute-start.1 = (bf16[256,1536]{1,0:T(8,128)(2,1)S(1)}, bf16[256,1536]{1,0:T(8,128)(2,1)S(1)}, u32[]{:S(2)}, u32[]{:S(2)}) collective-permute-start(bf16[256,1536]{1,0:T(8,128)(2,1)S(1)} %fusion.16), channel_id=1, source_target_pairs={{0,4},{2,6},{4,0},{6,2},{8,12},{10,14},{12,8},{14,10},{16,20},{18,... | collective-permute-start | bytes 2359304 | tf_op jit(solution)/shard_map/ppermute | solution.py:13
  71.7 39.8 %collective-permute-start.2 = (bf16[256,1536]{1,0:T(8,128)(2,1)S(1)}, bf16[256,1536]{1,0:T(8,128)(2,1)S(1)}, u32[]{:S(2)}, u32[]{:S(2)}) collective-permute-start(bf16[256,1536]{1,0:T(8,128)(2,1)S(1)} %fusion.17), channel_id=1, source_target_pairs={{0,8},{2,10},{4,12},{6,14},{8,0},{10,2},{12,4},{14,6},{16,24},{18,... | collective-permute-start | bytes 2359304 | tf_op jit(solution)/shard_map/ppermute | solution.py:13
  123.5 40.9 %collective-permute-start.3 = (bf16[256,1536]{1,0:T(8,128)(2,1)S(1)}, bf16[256,1536]{1,0:T(8,128)(2,1)S(1)}, u32[]{:S(2)}, u32[]{:S(2)}) collective-permute-start(bf16[256,1536]{1,0:T(8,128)(2,1)S(1)} %fusion.18), channel_id=1, source_target_pairs={{0,16},{2,18},{4,20},{6,22},{8,24},{10,26},{12,28},{14,30},{16,0},... | collective-permute-start | bytes 2359304 | tf_op jit(solution)/shard_map/ppermute | solution.py:13
  175.3 17.0 %collective-permute-start.4 = (bf16[256,1536]{1,0:T(8,128)(2,1)S(1)}, bf16[256,1536]{1,0:T(8,128)(2,1)S(1)}, u32[]{:S(2)}, u32[]{:S(2)}) collective-permute-start(bf16[256,1536]{1,0:T(8,128)(2,1)S(1)} %fusion.19), channel_id=1, source_target_pairs={{0,32},{2,34},{4,36},{6,38},{8,40},{10,42},{12,44},{14,46},{16,48}... | collective-permute-start | bytes 2359304 | tf_op jit(solution)/shard_map/ppermute | solution.py:13
  203.2 16.5 %collective-permute-start.5 = (bf16[256,1536]{1,0:T(8,128)(2,1)S(1)}, bf16[256,1536]{1,0:T(8,128)(2,1)S(1)}, u32[]{:S(2)}, u32[]{:S(2)}) collective-permute-start(bf16[256,1536]{1,0:T(8,128)(2,1)S(1)} %fusion.20), channel_id=1, source_target_pairs={{0,64},{2,66},{4,68},{6,70},{8,72},{10,74},{12,76},{14,78},{16,80}... | collective-permute-start | bytes 2359304 | tf_op jit(solution)/shard_map/ppermute | solution.py:13
  230.5 32.2 %collective-permute-start.6 = (bf16[256,1536]{1,0:T(8,128)(2,1)S(1)}, bf16[256,1536]{1,0:T(8,128)(2,1)S(1)}, u32[]{:S(2)}, u32[]{:S(2)}) collective-permute-start(bf16[256,1536]{1,0:T(8,128)(2,1)S(1)} %fusion.21), channel_id=1, source_target_pairs={{0,128},{2,130},{4,132},{6,134},{8,136},{10,138},{12,140},{14,142}... | collective-permute-start | bytes 2359304 | tf_op jit(solution)/shard_map/ppermute | solution.py:13
  278.1 42.1 %collective-permute-start.7 = (bf16[256,1536]{1,0:T(8,128)(2,1)S(1)}, bf16[256,1536]{1,0:T(8,128)(2,1)S(1)}, u32[]{:S(2)}, u32[]{:S(2)}) collective-permute-start(bf16[256,1536]{1,0:T(8,128)(2,1)S(1)} %fusion.22), channel_id=1, source_target_pairs={{0,256},{2,258},{4,260},{6,262},{8,264},{10,266},{12,268},{14,270}... | collective-permute-start | bytes 2359304 | tf_op jit(solution)/shard_map/ppermute | solution.py:13
where the time goes:
time: 365 us; the launch traced here: 361 us
  waiting for transfers between devices  160 us (44%)
  blocking collectives  138 us (38%)
  starting transfers between devices  50.1 us (14%)
  matrix products  6.84 us (2%)
  local copies, waits for them, and re-layouts  4.93 us (1%)
    ppermute x8, waiting for transfers between devices, from_partner(): lax.ppermute(x, axis, [(i, i ^ 1 << stride) for i in range(lax.axis_size(...  160 us
    all_gather x8, blocking collectives, over_pieces(): return lax.all_gather(x, axis).sum(0)  99.4 us
    ppermute x8, starting transfers between devices, from_partner(): lax.ppermute(x, axis, [(i, i ^ 1 << stride) for i in range(lax.axis_size(...  50.1 us
    all_to_all x1, blocking collectives, local(): lax.all_to_all(feature_part, 'slab', split_axis=0, concat_axis=1, tiled=T...  22.8 us
    all_to_all x1, blocking collectives, local(): lax.all_to_all(current, 'slab', split_axis=1, concat_axis=0, tiled=True)  15.5 us
  transfers between devices with their start and end apart: 8, of which 8 were waited for; matrix products, arithmetic and copies ran while one was open for 0% of the time, Pallas kernels for 0%

commit v1 on v0

v1 whole, which is shorter than its diff:
```python
import functools
import math

import jax
import jax.numpy as jnp
from jax import lax
from jax.experimental import pallas as pl
from jax.experimental.pallas import tpu as pltpu
from jax.sharding import PartitionSpec as P

D = 3072
N = 256
H = N // 2
F = D // 2
MESH = pl.DeviceIdType.MESH
NEAR, Z0, Z1, Z2, X0, X1, Y0, Y1 = range(8)


def layout(counts):
    at, out = 0, {}
    for name, count in counts:
        out[name] = at
        at += count
    return out, at


SEM, N_SEM = layout([
    ("near_raw", 1), ("in", 16), ("z_raw", 2), ("z_fwd", 16), ("perm", 8),
    ("p2", 4), ("p3z", 8), ("p3x", 4), ("p3f", 8),
    ("p4x", 4), ("p4y", 4), ("p4fx", 2), ("p4fy", 2), ("p5", 4), ("out", 2),
    ("cost", 11 * 4),
])


def kernel(w_hbm, p_ref, o_ref, wv, perms, raw, first, cur, got, mine_g, near_g, mix, ssem, rsem, lsem):
    rep, h = lax.axis_index("rep"), lax.axis_index("slab")
    g = rep % 2
    far = 1 - h

    def flip(bit):
        return rep + (1 << bit) * (1 - 2 * ((rep // (1 << bit)) % 2))

    def core(base, c):
        return base - g + c

    def xor(a, b):
        return a + b - 2 * a * b

    near = (flip(0), h)
    chip = [flip(b) for b in range(8)]
    same = [(chip[b], h) for b in range(8)]

    load = pltpu.make_async_copy(w_hbm.at[0], wv, lsem.at[0])
    load.start()

    peers = [near] + [same[b] for b in (Z1, Z2, X1, Y1)]
    for c in range(2):
        peers.append((core(rep, c), far))
        for b in (Z0, X0, Y0):
            peers.append((core(chip[b], c), h))
    barrier = pltpu.get_barrier_semaphore()
    for peer in peers:
        pl.semaphore_signal(barrier, inc=1, device_id=peer, device_id_type=MESH)
    pl.semaphore_wait(barrier, len(peers))

    sent = []

    def send(src, dst, sem, device):
        copy = pltpu.make_async_remote_copy(
            src_ref=src, dst_ref=dst, send_sem=ssem.at[sem], recv_sem=rsem.at[sem],
            device_id=device, device_id_type=MESH,
        )
        copy.start()
        sent.append(copy)

    def arrived(dst, sem):
        pltpu.make_async_remote_copy(
            src_ref=dst, dst_ref=dst, send_sem=ssem.at[0], recv_sem=rsem.at[sem],
            device_id=near, device_id_type=MESH,
        ).wait_recv()

    def half(c):
        return pl.ds(c * F, F)

    slot, far_slot = xor(g, h), xor(g, far)
    my_rows, far_rows = h * H, far * H
    step = H // 8

    load.wait()
    keep = pltpu.make_async_copy(
        wv.at[:, pl.ds(pl.multiple_of(g * F, F), F)],
        raw.at[0, slot, pl.ds(pl.multiple_of(my_rows, H), H)], lsem.at[1])
    keep.start()

    def send_in(q, c):
        src = wv.at[pl.ds(q * step, step), half(c)]
        dst = raw.at[0, far_slot, pl.ds(pl.multiple_of(my_rows + q * step, step), step)]
        copy = pltpu.make_async_remote_copy(
            src_ref=src, dst_ref=dst, send_sem=ssem.at[SEM["in"] + q * 2 + c],
            recv_sem=rsem.at[SEM["in"] + q * 2 + far_slot],
            device_id=(core(rep, c), far), device_id_type=MESH)
        copy.start()
        sent.append(copy)

    for q in range(8):
        for c in range(2):
            send_in(q, c)
    for c in range(2):
        copy = pltpu.make_async_remote_copy(
            src_ref=wv.at[:, half(c)],
            dst_ref=raw.at[1, slot, pl.ds(pl.multiple_of(my_rows, H), H)],
            send_sem=ssem.at[SEM["z_raw"] + c], recv_sem=rsem.at[SEM["z_raw"] + slot],
            device_id=(core(chip[Z0], c), h), device_id_type=MESH)
        copy.start()
        sent.append(copy)
    send(wv.at[:, pl.ds(pl.multiple_of((1 - g) * F, F), F)],
         raw.at[0, slot, pl.ds(pl.multiple_of(my_rows, H), H)], SEM["near_raw"], near)

    perms[0, slot] = p_ref[0]
    perm_to = [(0, near, 0)]
    for at, b in ((1, Z0), (2, X0), (3, Y0)):
        for c in range(2):
            perm_to.append((at, (core(chip[b], c), h), c))
    for at, device, c in perm_to:
        copy = pltpu.make_async_remote_copy(
            src_ref=p_ref.at[0], dst_ref=perms.at[at, slot],
            send_sem=ssem.at[SEM["perm"] + at * 2 + c], recv_sem=rsem.at[SEM["perm"] + at * 2 + slot],
            device_id=device, device_id_type=MESH)
        copy.start()
        sent.append(copy)

    for q in range(8):
        for s in range(2):
            rows = pl.ds(pl.multiple_of(far_rows + q * step, step), step)
            arrived(raw.at[0, s, rows], SEM["in"] + q * 2 + s)
            send(raw.at[0, s, rows], raw.at[1, s, rows], SEM["z_fwd"] + q * 2 + s, same[Z0])

    keep.wait()
    arrived(raw.at[0, 1 - slot, pl.ds(pl.multiple_of(my_rows, H), H)], SEM["near_raw"])
    arrived(perms.at[0, 1 - slot], SEM["perm"] + (1 - slot))
    for at in range(1, 4):
        for s in range(2):
            arrived(perms.at[at, s], SEM["perm"] + at * 2 + s)

    Q = N // 4

    def rows4(q):
        return pl.ds(q * Q, Q)

    def cost_part(level, q, part, own):
        mine_g[level, rows4(q)] = lax.dot_general(
            part[rows4(q)], own[...], (((1,), (1,)), ((), ())), preferred_element_type=jnp.float32)
        send(mine_g.at[level, rows4(q)], near_g.at[level, rows4(q)], SEM["cost"] + level * 4 + q, near)

    def merge(level, perm_row, part, own, out, then=lambda q: None):
        for q in range(4):
            arrived(near_g.at[level, rows4(q)], SEM["cost"] + level * 4 + q)
        cost = (mine_g[level] + near_g[level]) * (1.0 / math.sqrt(D))
        squared = cost * cost
        fourth = squared * squared
        scale = 1.0 / (1.0 + jnp.sum(fourth, axis=0, keepdims=True))
        neuron = lax.broadcasted_iota(jnp.int32, (N, N), 0)
        onehot = (neuron == perm_row).astype(jnp.float32)
        mixing = onehot + fourth * scale
        mix[...] = mixing.T.astype(jnp.bfloat16)
        for q in range(4):
            aligned = 0.5 * jnp.dot(mix[rows4(q)], part[...], preferred_element_type=jnp.float32)
            out[rows4(q)] = (
                (own[rows4(q)].astype(jnp.float32) + aligned) * (1.0 / math.sqrt(2.0))).astype(jnp.bfloat16)
            then(q)

    def perm_of(at, r):
        return perms[at, 0, r:r + 1]

    for q in range(4):
        cost_part(0, q, raw.at[0, 1], raw.at[0, 0])
    for s in range(2):
        arrived(raw.at[1, s, pl.ds(pl.multiple_of(my_rows, H), H)], SEM["z_raw"] + s)
    for q in range(8):
        for s in range(2):
            rows = pl.ds(pl.multiple_of(far_rows + q * step, step), step)
            arrived(raw.at[1, s, rows], SEM["z_fwd"] + q * 2 + s)
    for q in range(4):
        cost_part(1, q, raw.at[1, 1], raw.at[1, 0])
    merge(0, perm_of(0, 0), raw.at[0, 1], raw.at[0, 0], first.at[0])
    merge(1, perm_of(1, 0), raw.at[1, 1], raw.at[1, 0], first.at[1])
    for q in range(4):
        cost_part(2, q, first.at[1], first.at[0])

    def send2(q):
        send(cur.at[0, rows4(q)], got.at[0, rows4(q)], SEM["p2"] + q, same[Z1])

    merge(2, perm_of(0, 1), first.at[1], first.at[0], cur.at[0], send2)
    for q in range(4):
        arrived(got.at[0, rows4(q)], SEM["p2"] + q)
        cost_part(3, q, got.at[0], cur.at[0])

    O = N // 8

    def rows8(q):
        return pl.ds(q * O, O)

    def send3(q):
        for e in (2 * q, 2 * q + 1):
            send(cur.at[1, rows8(e)], got.at[1, rows8(e)], SEM["p3z"] + e, same[Z2])
        send(cur.at[1, rows4(q)], got.at[2, rows4(q)], SEM["p3x"] + q, same[X0])

    merge(3, perm_of(0, 2), got.at[0], cur.at[0], cur.at[1], send3)
    for q in range(4):
        for e in (2 * q, 2 * q + 1):
            arrived(got.at[1, rows8(e)], SEM["p3z"] + e)
            send(got.at[1, rows8(e)], got.at[3, rows8(e)], SEM["p3f"] + e, same[X0])
        cost_part(4, q, got.at[1], cur.at[1])
    for q in range(4):
        arrived(got.at[2, rows4(q)], SEM["p3x"] + q)
    for q in range(4):
        for e in (2 * q, 2 * q + 1):
            arrived(got.at[3, rows8(e)], SEM["p3f"] + e)
        cost_part(5, q, got.at[3], got.at[2])
    merge(4, perm_of(0, 3), got.at[1], cur.at[1], first.at[2])
    merge(5, perm_of(2, 3), got.at[3], got.at[2], first.at[3])
    for q in range(4):
        cost_part(6, q, first.at[3], first.at[2])

    def send4(q):
        send(cur.at[2, rows4(q)], got.at[5, rows4(q)], SEM["p4y"] + q, same[Y0])
        if q >= 2:
            send(cur.at[2, rows4(q)], got.at[4, rows4(q)], SEM["p4x"] + q, same[X1])
        if q == 3:
            for e in range(2):
                send(cur.at[2, rows4(e)], got.at[4, rows4(e)], SEM["p4x"] + e, same[X1])

    merge(6, perm_of(0, 4), first.at[3], first.at[2], cur.at[2], send4)
    for e in range(2):
        arrived(got.at[5, rows4(e)], SEM["p4y"] + e)
        send(got.at[5, rows4(e)], got.at[6, rows4(e)], SEM["p4fx"] + e, same[X1])
        arrived(got.at[4, rows4(e + 2)], SEM["p4x"] + e + 2)
        send(got.at[4, rows4(e + 2)], got.at[6, rows4(e + 2)], SEM["p4fy"] + e, same[Y0])
        cost_part(7, e + 2, got.at[4], cur.at[2])
    for e in range(2):
        arrived(got.at[4, rows4(e)], SEM["p4x"] + e)
        cost_part(7, e, got.at[4], cur.at[2])
        arrived(got.at[5, rows4(e + 2)], SEM["p4y"] + e + 2)
    for e in range(2):
        arrived(got.at[6, rows4(e)], SEM["p4fx"] + e)
        cost_part(8, e, got.at[6], got.at[5])
        arrived(got.at[6, rows4(e + 2)], SEM["p4fy"] + e)
        cost_part(8, e + 2, got.at[6], got.at[5])
    merge(7, perm_of(0, 5), got.at[4], cur.at[2], first.at[4])
    merge(8, perm_of(3, 5), got.at[6], got.at[5], first.at[5])
    for q in range(4):
        cost_part(9, q, first.at[5], first.at[4])

    def send5(q):
        send(cur.at[3, rows4(q)], got.at[7, rows4(q)], SEM["p5"] + q, same[Y1])

    merge(9, perm_of(0, 6), first.at[5], first.at[4], cur.at[3], send5)
    for q in range(4):
        arrived(got.at[7, rows4(q)], SEM["p5"] + q)
        cost_part(10, q, got.at[7], cur.at[3])
    fin = first.at[6]
    merge(10, perm_of(0, 7), got.at[7], cur.at[3], fin)

    cols = pl.ds(pl.multiple_of(g * F, F), F)
    away = pltpu.make_async_remote_copy(
        src_ref=fin.at[pl.ds(pl.multiple_of(far_rows, H), H)], dst_ref=o_ref.at[0, :, cols],
        send_sem=ssem.at[SEM["out"]], recv_sem=rsem.at[SEM["out"] + g],
        device_id=(core(rep, h), far), device_id_type=MESH)
    away.start()
    home_src = fin.at[pl.ds(pl.multiple_of(my_rows, H), H)]

    @pl.when(slot == 0)
    def _():
        home = pltpu.make_async_copy(home_src, o_ref.at[0, :, cols], lsem.at[2])
        home.start()
        home.wait()
        arrived(o_ref.at[0, :, pl.ds(pl.multiple_of((1 - g) * F, F), F)], SEM["out"] + 1 - g)

    @pl.when(slot == 1)
    def _():
        home = pltpu.make_async_remote_copy(
            src_ref=home_src, dst_ref=o_ref.at[0, :, cols],
            send_sem=ssem.at[SEM["out"] + 1], recv_sem=rsem.at[SEM["out"] + g],
            device_id=near, device_id_type=MESH)
        home.start()
        for c in range(2):
            arrived(o_ref.at[0, :, half(c)], SEM["out"] + c)
        home.wait_send()

    away.wait_send()
    for copy in sent:
        copy.wait_send()


def local(weights, perms):
    rows = (N, F)
    return pl.pallas_call(
        kernel,
        out_shape=jax.ShapeDtypeStruct((1, H, D), jnp.bfloat16),
        in_specs=[pl.BlockSpec(memory_space=pl.ANY), pl.BlockSpec(memory_space=pltpu.VMEM)],
        out_specs=pl.BlockSpec(memory_space=pl.ANY),
        scratch_shapes=[
            pltpu.VMEM((H, D), jnp.bfloat16),
            pltpu.VMEM((4, 2, 8, N), jnp.int32),
            pltpu.VMEM((2, 2, *rows), jnp.bfloat16),
            pltpu.VMEM((7, *rows), jnp.bfloat16),
            pltpu.VMEM((4, *rows), jnp.bfloat16),
            pltpu.VMEM((8, *rows), jnp.bfloat16),
            pltpu.VMEM((11, N, N), jnp.float32),
            pltpu.VMEM((11, N, N), jnp.float32),
            pltpu.VMEM((N, N), jnp.bfloat16),
            pltpu.SemaphoreType.DMA((N_SEM,)),
            pltpu.SemaphoreType.DMA((N_SEM,)),
            pltpu.SemaphoreType.DMA((3,)),
        ],
        compiler_params=pltpu.CompilerParams(
            collective_id=0, has_side_effects=True, vmem_limit_bytes=60 * 1024 * 1024),
    )(weights, perms)


def solution(mesh):
    placed = (P("rep", "slab", None), P("rep", None, None))
    return jax.shard_map(
        local, mesh=mesh, in_specs=placed, out_specs=P("rep", "slab", None), check_vma=False
    )
```

time: 365 us -> 280 us (0.77)
  the two profiles are of different devices: /device:TPU:57 before, /device:TPU:60 now
where the time goes in v1:
time: 280 us
  Pallas kernels  278 us (99%)
    pallas_call x1, Pallas kernels, local(): pl.pallas_call(kernel, out_shape=jax.ShapeDtypeStruct((1, H, D), jnp.bflo...  278 us

profile of v1, /device:TPU:60, one launch (start us, length us, event | category | flops | bytes accessed | tf_op | source)
XLA Modules:
  0.0 279.8 jit_solution(15664760595575180266)
XLA Ops:
  0.0 277.8 %shard_map.28 = bf16[1,128,3072]{2,1,0:T(8,128)(2,1)} custom-call(bf16[1,128,3072]{2,1,0:T(8,128)(2,1)} %w_hbm.1, s32[1,8,256]{2,1,0:T(8,128)} %p_ref.1), custom_call_target="tpu_custom_call" | custom-call | tf_op jit(solution)/shard_map/pallas_call | solution.py:297
  277.8 2.1 copy.4

commit v2 on v1

--- a/solution.py
+++ b/solution.py
@@ -26,13 +26,12 @@
 
 SEM, N_SEM = layout([
     ("near_raw", 1), ("in", 16), ("z_raw", 2), ("z_fwd", 16), ("perm", 8),
-    ("p2", 4), ("p3z", 8), ("p3x", 4), ("p3f", 8),
-    ("p4x", 4), ("p4y", 4), ("p4fx", 2), ("p4fy", 2), ("p5", 4), ("out", 2),
+    ("z1", 8), ("z2", 8), ("z3", 4), ("z4", 4), ("x1", 8), ("x2", 4), ("y0", 4), ("y1", 4), ("out", 2),
     ("cost", 11 * 4),
 ])
 
 
-def kernel(w_hbm, p_ref, o_ref, wv, perms, raw, first, cur, got, mine_g, near_g, mix, ssem, rsem, lsem):
+def kernel(w_hbm, p_ref, o_ref, wv, perms, raw, first, cur, got, relay, relay_half, mine_g, near_g, mix, ssem, rsem, lsem):
     rep, h = lax.axis_index("rep"), lax.axis_index("slab")
     g = rep % 2
     far = 1 - h
@@ -53,10 +52,14 @@
     load = pltpu.make_async_copy(w_hbm.at[0], wv, lsem.at[0])
     load.start()
 
-    peers = [near] + [same[b] for b in (Z1, Z2, X1, Y1)]
+    z, x = (rep // 2) % 8, (rep // 16) % 4
+    z_next, z_last = (rep + 2 * ((z + 1) % 8 - z), h), (rep + 2 * ((z + 7) % 8 - z), h)
+    x_next, x_last = (rep + 16 * ((x + 1) % 4 - x), h), (rep + 16 * ((x + 3) % 4 - x), h)
+
+    peers = [near, z_next, z_last, x_next, x_last, same[Y0], same[Y1]]
     for c in range(2):
         peers.append((core(rep, c), far))
-        for b in (Z0, X0, Y0):
+        for b in (Z0, Z2, X1):
             peers.append((core(chip[b], c), h))
     barrier = pltpu.get_barrier_semaphore()
     for peer in peers:
@@ -118,7 +121,7 @@
 
     perms[0, slot] = p_ref[0]
     perm_to = [(0, near, 0)]
-    for at, b in ((1, Z0), (2, X0), (3, Y0)):
+    for at, b in ((1, Z0), (2, Z2), (3, X1)):
         for c in range(2):
             perm_to.append((at, (core(chip[b], c), h), c))
     for at, device, c in perm_to:
@@ -187,76 +190,89 @@
     for q in range(4):
         cost_part(2, q, first.at[1], first.at[0])
 
-    def send2(q):
-        send(cur.at[0, rows4(q)], got.at[0, rows4(q)], SEM["p2"] + q, same[Z1])
-
-    merge(2, perm_of(0, 1), first.at[1], first.at[0], cur.at[0], send2)
-    for q in range(4):
-        arrived(got.at[0, rows4(q)], SEM["p2"] + q)
-        cost_part(3, q, got.at[0], cur.at[0])
-
-    O = N // 8
-
-    def rows8(q):
-        return pl.ds(q * O, O)
-
-    def send3(q):
-        for e in (2 * q, 2 * q + 1):
-            send(cur.at[1, rows8(e)], got.at[1, rows8(e)], SEM["p3z"] + e, same[Z2])
-        send(cur.at[1, rows4(q)], got.at[2, rows4(q)], SEM["p3x"] + q, same[X0])
-
-    merge(3, perm_of(0, 2), got.at[0], cur.at[0], cur.at[1], send3)
-    for q in range(4):
-        for e in (2 * q, 2 * q + 1):
-            arrived(got.at[1, rows8(e)], SEM["p3z"] + e)
-            send(got.at[1, rows8(e)], got.at[3, rows8(e)], SEM["p3f"] + e, same[X0])
-        cost_part(4, q, got.at[1], cur.at[1])
-    for q in range(4):
-        arrived(got.at[2, rows4(q)], SEM["p3x"] + q)
-    for q in range(4):
-        for e in (2 * q, 2 * q + 1):
-            arrived(got.at[3, rows8(e)], SEM["p3f"] + e)
-        cost_part(5, q, got.at[3], got.at[2])
-    merge(4, perm_of(0, 3), got.at[1], cur.at[1], first.at[2])
-    merge(5, perm_of(2, 3), got.at[3], got.at[2], first.at[3])
-    for q in range(4):
-        cost_part(6, q, first.at[3], first.at[2])
-
-    def send4(q):
-        send(cur.at[2, rows4(q)], got.at[5, rows4(q)], SEM["p4y"] + q, same[Y0])
+    def quad(level, at, r, own, slots, wait_rings, wait_last, tmp, out, then):
+        for q in range(4):
+            wait_rings(q)
+            cost_part(level, q, slots.at[0], own)
+        wait_last()
+        for q in range(4):
+            cost_part(level + 1, q, slots.at[2], slots.at[1])
+        merge(level, perm_of(0, r), slots.at[0], own, tmp.at[0])
+        merge(level + 1, perm_of(at, r), slots.at[2], slots.at[1], tmp.at[1])
+        for q in range(4):
+            cost_part(level + 2, q, tmp.at[1], tmp.at[0])
+        merge(level + 2, perm_of(0, r + 1), tmp.at[1], tmp.at[0], out, then)
+
+    zq = got.at[pl.ds(0, 3)]
+
+    def bit1(v):
+        return (v // 2) % 2
+
+    def send_z1(q):
+        send(cur.at[0, rows4(q)], relay.at[0, rows4(q)], SEM["z1"] + q, z_next)
+        send(cur.at[0, rows4(q)], relay.at[1, rows4(q)], SEM["z1"] + 4 + q, z_last)
+
+    to_next, to_last = 2 * (1 - bit1((z + 1) % 8)), 2 * bit1((z + 7) % 8)
+    from_last, from_next = 2 * (1 - bit1(z)), 2 * bit1(z)
+
+    merge(2, perm_of(0, 1), first.at[1], first.at[0], cur.at[0], send_z1)
+    for q in range(4):
+        arrived(relay.at[0, rows4(q)], SEM["z1"] + q)
+        send(relay.at[0, rows4(q)], zq.at[to_next, rows4(q)], SEM["z2"] + q, z_next)
+        arrived(relay.at[1, rows4(q)], SEM["z1"] + 4 + q)
+        send(relay.at[1, rows4(q)], zq.at[to_last, rows4(q)], SEM["z2"] + 4 + q, z_last)
+
+    def rings_z(q):
+        arrived(zq.at[from_last, rows4(q)], SEM["z2"] + q)
+        if q < 2:
+            send(zq.at[from_last, rows4(q)], relay_half.at[0, rows4(q)], SEM["z3"] + q, z_next)
+        arrived(zq.at[from_next, rows4(q)], SEM["z2"] + 4 + q)
         if q >= 2:
-            send(cur.at[2, rows4(q)], got.at[4, rows4(q)], SEM["p4x"] + q, same[X1])
-        if q == 3:
-            for e in range(2):
-                send(cur.at[2, rows4(e)], got.at[4, rows4(e)], SEM["p4x"] + e, same[X1])
-
-    merge(6, perm_of(0, 4), first.at[3], first.at[2], cur.at[2], send4)
-    for e in range(2):
-        arrived(got.at[5, rows4(e)], SEM["p4y"] + e)
-        send(got.at[5, rows4(e)], got.at[6, rows4(e)], SEM["p4fx"] + e, same[X1])
-        arrived(got.at[4, rows4(e + 2)], SEM["p4x"] + e + 2)
-        send(got.at[4, rows4(e + 2)], got.at[6, rows4(e + 2)], SEM["p4fy"] + e, same[Y0])
-        cost_part(7, e + 2, got.at[4], cur.at[2])
-    for e in range(2):
-        arrived(got.at[4, rows4(e)], SEM["p4x"] + e)
-        cost_part(7, e, got.at[4], cur.at[2])
-        arrived(got.at[5, rows4(e + 2)], SEM["p4y"] + e + 2)
-    for e in range(2):
-        arrived(got.at[6, rows4(e)], SEM["p4fx"] + e)
-        cost_part(8, e, got.at[6], got.at[5])
-        arrived(got.at[6, rows4(e + 2)], SEM["p4fy"] + e)
-        cost_part(8, e + 2, got.at[6], got.at[5])
-    merge(7, perm_of(0, 5), got.at[4], cur.at[2], first.at[4])
-    merge(8, perm_of(3, 5), got.at[6], got.at[5], first.at[5])
-    for q in range(4):
-        cost_part(9, q, first.at[5], first.at[4])
-
-    def send5(q):
-        send(cur.at[3, rows4(q)], got.at[7, rows4(q)], SEM["p5"] + q, same[Y1])
-
-    merge(9, perm_of(0, 6), first.at[5], first.at[4], cur.at[3], send5)
-    for q in range(4):
-        arrived(got.at[7, rows4(q)], SEM["p5"] + q)
+            send(zq.at[from_next, rows4(q)], relay_half.at[1, rows4(q - 2)], SEM["z3"] + q, z_last)
+
+    def last_z():
+        for q in range(2):
+            arrived(relay_half.at[0, rows4(q)], SEM["z3"] + q)
+            send(relay_half.at[0, rows4(q)], zq.at[1, rows4(q)], SEM["z4"] + q, z_next)
+            arrived(relay_half.at[1, rows4(q)], SEM["z3"] + 2 + q)
+            send(relay_half.at[1, rows4(q)], zq.at[1, rows4(q + 2)], SEM["z4"] + 2 + q, z_last)
+        for q in range(4):
+            arrived(zq.at[1, rows4(q)], SEM["z4"] + q)
+
+    def send_x1(q):
+        send(cur.at[1, rows4(q)], xq.at[2 * (x % 2), rows4(q)], SEM["x1"] + q, x_next)
+        send(cur.at[1, rows4(q)], xq.at[2 * (1 - x % 2), rows4(q)], SEM["x1"] + 4 + q, x_last)
+
+    xq = got.at[pl.ds(3, 3)]
+    quad(3, 2, 2, cur.at[0], zq, rings_z, last_z, first.at[pl.ds(2, 2)], cur.at[1], send_x1)
+
+    def rings_x(q):
+        arrived(xq.at[2 * (1 - x % 2), rows4(q)], SEM["x1"] + q)
+        if q < 2:
+            send(xq.at[2 * (1 - x % 2), rows4(q)], xq.at[1, rows4(q)], SEM["x2"] + q, x_next)
+        arrived(xq.at[2 * (x % 2), rows4(q)], SEM["x1"] + 4 + q)
+        if q >= 2:
+            send(xq.at[2 * (x % 2), rows4(q)], xq.at[1, rows4(q)], SEM["x2"] + q, x_last)
+
+    def last_x():
+        for q in range(4):
+            arrived(xq.at[1, rows4(q)], SEM["x2"] + q)
+
+    def send_y0(q):
+        send(cur.at[2, rows4(q)], got.at[6, rows4(q)], SEM["y0"] + q, same[Y0])
+
+    quad(6, 3, 4, cur.at[1], xq, rings_x, last_x, first.at[pl.ds(4, 2)], cur.at[2], send_y0)
+
+    for q in range(4):
+        arrived(got.at[6, rows4(q)], SEM["y0"] + q)
+        cost_part(9, q, got.at[6], cur.at[2])
+
+    def send_y1(q):
+        send(cur.at[3, rows4(q)], got.at[7, rows4(q)], SEM["y1"] + q, same[Y1])
+
+    merge(9, perm_of(0, 6), got.at[6], cur.at[2], cur.at[3], send_y1)
+    for q in range(4):
+        arrived(got.at[7, rows4(q)], SEM["y1"] + q)
         cost_part(10, q, got.at[7], cur.at[3])
     fin = first.at[6]
     merge(10, perm_of(0, 7), got.at[7], cur.at[3], fin)
@@ -306,6 +322,8 @@
             pltpu.VMEM((7, *rows), jnp.bfloat16),
             pltpu.VMEM((4, *rows), jnp.bfloat16),
             pltpu.VMEM((8, *rows), jnp.bfloat16),
+            pltpu.VMEM((2, *rows), jnp.bfloat16),
+            pltpu.VMEM((2, H, F), jnp.bfloat16),
             pltpu.VMEM((11, N, N), jnp.float32),
             pltpu.VMEM((11, N, N), jnp.float32),
             pltpu.VMEM((N, N), jnp.bfloat16),

time: 280 us -> 249 us (0.89)
  the two profiles are of different devices: /device:TPU:60 before, /device:TPU:25 now
where the time goes in v2:
time: 249 us
  Pallas kernels  247 us (99%)
    pallas_call x1, Pallas kernels, local(): pl.pallas_call(kernel, out_shape=jax.ShapeDtypeStruct((1, H, D), jnp.bflo...  247 us

profile of v2, /device:TPU:25, one launch (start us, length us, event | category | flops | bytes accessed | tf_op | source)
XLA Modules:
  0.0 249.2 jit_solution(10655707888438451882)
XLA Ops:
  0.0 247.1 %shard_map.28 = bf16[1,128,3072]{2,1,0:T(8,128)(2,1)} custom-call(bf16[1,128,3072]{2,1,0:T(8,128)(2,1)} %w_hbm.1, s32[1,8,256]{2,1,0:T(8,128)} %p_ref.1), custom_call_target="tpu_custom_call" | custom-call | tf_op jit(solution)/shard_map/pallas_call | solution.py:313
  247.1 2.1 copy.4

commit v3 on v2

--- a/solution.py
+++ b/solution.py
@@ -25,9 +25,9 @@
 
 
 SEM, N_SEM = layout([
-    ("near_raw", 1), ("in", 16), ("z_raw", 2), ("z_fwd", 16), ("perm", 8),
-    ("z1", 8), ("z2", 8), ("z3", 4), ("z4", 4), ("x1", 8), ("x2", 4), ("y0", 4), ("y1", 4), ("out", 2),
-    ("cost", 11 * 4),
+    ("near_raw", 1), ("in", 16), ("z_raw", 2), ("z_fwd", 16), ("perm", 10),
+    ("z1", 8), ("z2", 8), ("z3", 4), ("z4", 4), ("x1", 8), ("x2", 4), ("y1", 4), ("y2", 4), ("y3", 4), ("out", 2), ("away", 4),
+    ("cost", 12 * 4),
 ])
 
 
@@ -56,10 +56,14 @@
     z_next, z_last = (rep + 2 * ((z + 1) % 8 - z), h), (rep + 2 * ((z + 7) % 8 - z), h)
     x_next, x_last = (rep + 16 * ((x + 1) % 4 - x), h), (rep + 16 * ((x + 3) % 4 - x), h)
 
-    peers = [near, z_next, z_last, x_next, x_last, same[Y0], same[Y1]]
+    y = (rep // 64) % 4
+    inner = ((y + 1) // 2) % 2
+    y_cross = (rep + 64 * (3 - 2 * y), h)
+    peers = [near, z_next, z_last, x_next, x_last, same[Y0], y_cross]
     for c in range(2):
         peers.append((core(rep, c), far))
-        for b in (Z0, Z2, X1):
+        peers.append((core(chip[Y1], c), far))
+        for b in (Z0, Z2, X1, Y1):
             peers.append((core(chip[b], c), h))
     barrier = pltpu.get_barrier_semaphore()
     for peer in peers:
@@ -121,7 +125,7 @@
 
     perms[0, slot] = p_ref[0]
     perm_to = [(0, near, 0)]
-    for at, b in ((1, Z0), (2, Z2), (3, X1)):
+    for at, b in ((1, Z0), (2, Z2), (3, X1), (4, Y1)):
         for c in range(2):
             perm_to.append((at, (core(chip[b], c), h), c))
     for at, device, c in perm_to:
@@ -141,7 +145,7 @@
     keep.wait()
     arrived(raw.at[0, 1 - slot, pl.ds(pl.multiple_of(my_rows, H), H)], SEM["near_raw"])
     arrived(perms.at[0, 1 - slot], SEM["perm"] + (1 - slot))
-    for at in range(1, 4):
+    for at in range(1, 5):
         for s in range(2):
             arrived(perms.at[at, s], SEM["perm"] + at * 2 + s)
 
@@ -150,58 +154,68 @@
     def rows4(q):
         return pl.ds(q * Q, Q)
 
-    def cost_part(level, q, part, own):
-        mine_g[level, rows4(q)] = lax.dot_general(
-            part[rows4(q)], own[...], (((1,), (1,)), ((), ())), preferred_element_type=jnp.float32)
-        send(mine_g.at[level, rows4(q)], near_g.at[level, rows4(q)], SEM["cost"] + level * 4 + q, near)
-
-    def merge(level, perm_row, part, own, out, then=lambda q: None):
-        for q in range(4):
-            arrived(near_g.at[level, rows4(q)], SEM["cost"] + level * 4 + q)
+    pieces = {}
+
+    def cost_part(level, q, part, own, parts=4):
+        pieces[level] = parts
+        rows = pl.ds(q * (N // parts), N // parts)
+        mine_g[level, rows] = lax.dot_general(
+            part[rows], own[...], (((1,), (1,)), ((), ())), preferred_element_type=jnp.float32)
+        send(mine_g.at[level, rows], near_g.at[level, rows], SEM["cost"] + level * 4 + q, near)
+
+    def fourth_of(level):
+        parts = pieces[level]
+        for q in range(parts):
+            arrived(near_g.at[level, pl.ds(q * (N // parts), N // parts)], SEM["cost"] + level * 4 + q)
         cost = (mine_g[level] + near_g[level]) * (1.0 / math.sqrt(D))
         squared = cost * cost
-        fourth = squared * squared
-        scale = 1.0 / (1.0 + jnp.sum(fourth, axis=0, keepdims=True))
+        return squared * squared
+
+    def onehot_of(perm_row):
         neuron = lax.broadcasted_iota(jnp.int32, (N, N), 0)
-        onehot = (neuron == perm_row).astype(jnp.float32)
-        mixing = onehot + fourth * scale
-        mix[...] = mixing.T.astype(jnp.bfloat16)
-        for q in range(4):
-            aligned = 0.5 * jnp.dot(mix[rows4(q)], part[...], preferred_element_type=jnp.float32)
-            out[rows4(q)] = (
-                (own[rows4(q)].astype(jnp.float32) + aligned) * (1.0 / math.sqrt(2.0))).astype(jnp.bfloat16)
+        return jnp.where(neuron == perm_row, 0.5, 0.0)
+
+    def mixing_of(fourth, perm_row):
+        scale = 0.5 / (1.0 + jnp.sum(fourth, axis=0, keepdims=True))
+        mix[...] = (onehot_of(perm_row) + fourth * scale).T.astype(jnp.bfloat16)
+
+    def mix_in(part, own, out, then):
+        for t in range(F // N):
+            tile = pl.ds(t * N, N)
+            aligned = jnp.dot(mix[...], part[:, tile], preferred_element_type=jnp.float32)
+            out[:, tile] = (
+                (own[:, tile].astype(jnp.float32) + aligned) * (1.0 / math.sqrt(2.0))).astype(jnp.bfloat16)
+        for q in range(4):
             then(q)
+
+    def merge(level, perm_row, part, own, out, then=lambda q: None):
+        mixing_of(fourth_of(level), perm_row)
+        mix_in(part, own, out, then)
 
     def perm_of(at, r):
         return perms[at, 0, r:r + 1]
 
-    for q in range(4):
-        cost_part(0, q, raw.at[0, 1], raw.at[0, 0])
+    cost_part(0, 0, raw.at[0, 1], raw.at[0, 0], 1)
+    merge(0, perm_of(0, 0), raw.at[0, 1], raw.at[0, 0], first.at[0])
     for s in range(2):
         arrived(raw.at[1, s, pl.ds(pl.multiple_of(my_rows, H), H)], SEM["z_raw"] + s)
     for q in range(8):
         for s in range(2):
             rows = pl.ds(pl.multiple_of(far_rows + q * step, step), step)
             arrived(raw.at[1, s, rows], SEM["z_fwd"] + q * 2 + s)
-    for q in range(4):
-        cost_part(1, q, raw.at[1, 1], raw.at[1, 0])
-    merge(0, perm_of(0, 0), raw.at[0, 1], raw.at[0, 0], first.at[0])
+    cost_part(1, 0, raw.at[1, 1], raw.at[1, 0], 1)
     merge(1, perm_of(1, 0), raw.at[1, 1], raw.at[1, 0], first.at[1])
-    for q in range(4):
-        cost_part(2, q, first.at[1], first.at[0])
-
-    def quad(level, at, r, own, slots, wait_rings, wait_last, tmp, out, then):
+    cost_part(2, 0, first.at[1], first.at[0], 1)
+
+    def quad(level, at, r, own, slots, wait_rings, wait_last, tmp):
         for q in range(4):
             wait_rings(q)
             cost_part(level, q, slots.at[0], own)
+        merge(level, perm_of(0, r), slots.at[0], own, tmp.at[0])
         wait_last()
-        for q in range(4):
-            cost_part(level + 1, q, slots.at[2], slots.at[1])
-        merge(level, perm_of(0, r), slots.at[0], own, tmp.at[0])
+        cost_part(level + 1, 0, slots.at[2], slots.at[1], 1)
         merge(level + 1, perm_of(at, r), slots.at[2], slots.at[1], tmp.at[1])
-        for q in range(4):
-            cost_part(level + 2, q, tmp.at[1], tmp.at[0])
-        merge(level + 2, perm_of(0, r + 1), tmp.at[1], tmp.at[0], out, then)
+        cost_part(level + 2, 0, tmp.at[1], tmp.at[0], 1)
 
     zq = got.at[pl.ds(0, 3)]
 
@@ -244,7 +258,8 @@
         send(cur.at[1, rows4(q)], xq.at[2 * (1 - x % 2), rows4(q)], SEM["x1"] + 4 + q, x_last)
 
     xq = got.at[pl.ds(3, 3)]
-    quad(3, 2, 2, cur.at[0], zq, rings_z, last_z, first.at[pl.ds(2, 2)], cur.at[1], send_x1)
+    quad(3, 2, 2, cur.at[0], zq, rings_z, last_z, first.at[pl.ds(2, 2)])
+    merge(5, perm_of(0, 3), first.at[3], first.at[2], cur.at[1], send_x1)
 
     def rings_x(q):
         arrived(xq.at[2 * (1 - x % 2), rows4(q)], SEM["x1"] + q)
@@ -258,52 +273,85 @@
         for q in range(4):
             arrived(xq.at[1, rows4(q)], SEM["x2"] + q)
 
-    def send_y0(q):
-        send(cur.at[2, rows4(q)], got.at[6, rows4(q)], SEM["y0"] + q, same[Y0])
-
-    quad(6, 3, 4, cur.at[1], xq, rings_x, last_x, first.at[pl.ds(4, 2)], cur.at[2], send_y0)
-
-    for q in range(4):
-        arrived(got.at[6, rows4(q)], SEM["y0"] + q)
-        cost_part(9, q, got.at[6], cur.at[2])
-
-    def send_y1(q):
-        send(cur.at[3, rows4(q)], got.at[7, rows4(q)], SEM["y1"] + q, same[Y1])
-
-    merge(9, perm_of(0, 6), got.at[6], cur.at[2], cur.at[3], send_y1)
-    for q in range(4):
-        arrived(got.at[7, rows4(q)], SEM["y1"] + q)
-        cost_part(10, q, got.at[7], cur.at[3])
-    fin = first.at[6]
-    merge(10, perm_of(0, 7), got.at[7], cur.at[3], fin)
-
-    cols = pl.ds(pl.multiple_of(g * F, F), F)
-    away = pltpu.make_async_remote_copy(
-        src_ref=fin.at[pl.ds(pl.multiple_of(far_rows, H), H)], dst_ref=o_ref.at[0, :, cols],
-        send_sem=ssem.at[SEM["out"]], recv_sem=rsem.at[SEM["out"] + g],
-        device_id=(core(rep, h), far), device_id_type=MESH)
-    away.start()
-    home_src = fin.at[pl.ds(pl.multiple_of(my_rows, H), H)]
-
-    @pl.when(slot == 0)
+    quad(6, 3, 4, cur.at[1], xq, rings_x, last_x, first.at[pl.ds(4, 2)])
+
+    yq = got.at[pl.ds(6, 3)]
+    o_cols = pl.ds(pl.multiple_of(g * F, F), F)
+
+    @pl.when(inner == 0)
     def _():
-        home = pltpu.make_async_copy(home_src, o_ref.at[0, :, cols], lsem.at[2])
-        home.start()
-        home.wait()
-        arrived(o_ref.at[0, :, pl.ds(pl.multiple_of((1 - g) * F, F), F)], SEM["out"] + 1 - g)
-
-    @pl.when(slot == 1)
-    def _():
-        home = pltpu.make_async_remote_copy(
-            src_ref=home_src, dst_ref=o_ref.at[0, :, cols],
-            send_sem=ssem.at[SEM["out"] + 1], recv_sem=rsem.at[SEM["out"] + g],
-            device_id=near, device_id_type=MESH)
-        home.start()
+        outer_sends = []
+        merge(8, perm_of(0, 5), first.at[5], first.at[4], cur.at[2])
+        for q in range(4):
+            copy = pltpu.make_async_remote_copy(
+                src_ref=cur.at[2, rows4(q)], dst_ref=yq.at[0, rows4(q)], send_sem=ssem.at[SEM["y1"] + q],
+                recv_sem=rsem.at[SEM["y1"] + q], device_id=same[Y0], device_id_type=MESH)
+            copy.start()
+            outer_sends.append(copy)
         for c in range(2):
             arrived(o_ref.at[0, :, half(c)], SEM["out"] + c)
-        home.wait_send()
-
-    away.wait_send()
+        for copy in outer_sends:
+            copy.wait_send()
+
+    @pl.when(inner == 1)
+    def _():
+        before = len(sent)
+
+        def send_y2(q):
+            send(cur.at[2, rows4(q)], yq.at[2, rows4(q)], SEM["y2"] + q, y_cross)
+
+        merge(8, perm_of(0, 5), first.at[5], first.at[4], cur.at[2], send_y2)
+
+        def rings_y(q):
+            arrived(yq.at[0, rows4(q)], SEM["y1"] + q)
+            send(yq.at[0, rows4(q)], yq.at[1, rows4(q)], SEM["y3"] + q, y_cross)
+
+        def last_y():
+            for q in range(4):
+                arrived(yq.at[2, rows4(q)], SEM["y2"] + q)
+            for q in range(4):
+                arrived(yq.at[1, rows4(q)], SEM["y3"] + q)
+
+        quad(9, 4, 6, cur.at[2], yq, rings_y, last_y, first.at[pl.ds(6, 2)])
+        ours, theirs = first.at[6], first.at[7]
+
+        def away(src, rows, at, device):
+            copy = pltpu.make_async_remote_copy(
+                src_ref=src.at[pl.ds(pl.multiple_of(rows, H), H)], dst_ref=o_ref.at[0, :, o_cols],
+                send_sem=ssem.at[SEM["away"] + at], recv_sem=rsem.at[SEM["out"] + g],
+                device_id=device, device_id_type=MESH)
+            copy.start()
+            return copy
+
+        fourth = fourth_of(11)
+        mixing_of(fourth, perm_of(0, 7))
+        mix_in(theirs, ours, cur.at[3], lambda q: None)
+        leaving = [away(cur.at[3], far_rows, 0, (core(rep, h), far))]
+        scale = 0.5 / (1.0 + jnp.sum(fourth, axis=1, keepdims=True))
+        mix[...] = (onehot_of(perm_of(4, 7)).T + fourth * scale).astype(jnp.bfloat16)
+        mix_in(ours, theirs, cur.at[4], lambda q: None)
+        leaving.append(away(cur.at[4], my_rows, 1, (core(chip[Y1], h), h)))
+        leaving.append(away(cur.at[4], far_rows, 2, (core(chip[Y1], h), far)))
+
+        @pl.when(slot == 0)
+        def _():
+            home = pltpu.make_async_copy(
+                cur.at[3, pl.ds(pl.multiple_of(my_rows, H), H)], o_ref.at[0, :, o_cols], lsem.at[2])
+            home.start()
+            home.wait()
+            arrived(o_ref.at[0, :, pl.ds(pl.multiple_of((1 - g) * F, F), F)], SEM["out"] + 1 - g)
+
+        @pl.when(slot == 1)
+        def _():
+            home = away(cur.at[3], my_rows, 3, near)
+            for c in range(2):
+                arrived(o_ref.at[0, :, half(c)], SEM["out"] + c)
+            home.wait_send()
+
+        for copy in leaving + sent[before:]:
+            copy.wait_send()
+        del sent[before:]
+
     for copy in sent:
         copy.wait_send()
 
@@ -317,15 +365,15 @@
         out_specs=pl.BlockSpec(memory_space=pl.ANY),
         scratch_shapes=[
             pltpu.VMEM((H, D), jnp.bfloat16),
-            pltpu.VMEM((4, 2, 8, N), jnp.int32),
+            pltpu.VMEM((5, 2, 8, N), jnp.int32),
             pltpu.VMEM((2, 2, *rows), jnp.bfloat16),
-            pltpu.VMEM((7, *rows), jnp.bfloat16),
-            pltpu.VMEM((4, *rows), jnp.bfloat16),
             pltpu.VMEM((8, *rows), jnp.bfloat16),
+            pltpu.VMEM((5, *rows), jnp.bfloat16),
+            pltpu.VMEM((9, *rows), jnp.bfloat16),
             pltpu.VMEM((2, *rows), jnp.bfloat16),
             pltpu.VMEM((2, H, F), jnp.bfloat16),
-            pltpu.VMEM((11, N, N), jnp.float32),
-            pltpu.VMEM((11, N, N), jnp.float32),
+            pltpu.VMEM((12, N, N), jnp.float32),
+            pltpu.VMEM((12, N, N), jnp.float32),
             pltpu.VMEM((N, N), jnp.bfloat16),
             pltpu.SemaphoreType.DMA((N_SEM,)),
             pltpu.SemaphoreType.DMA((N_SEM,)),

time: 249 us -> 222 us (0.89)
  the two profiles are of different devices: /device:TPU:25 before, /device:TPU:1 now
where the time goes in v3:
time: 222 us
  Pallas kernels  220 us (99%)
    pallas_call x1, Pallas kernels, local(): pl.pallas_call(kernel, out_shape=jax.ShapeDtypeStruct((1, H, D), jnp.bflo...  220 us

profile of v3, /device:TPU:1, one launch (start us, length us, event | category | flops | bytes accessed | tf_op | source)
XLA Modules:
  0.0 222.2 jit_solution(15122920079430363452)
XLA Ops:
  0.0 220.1 %shard_map.28 = bf16[1,128,3072]{2,1,0:T(8,128)(2,1)} custom-call(bf16[1,128,3072]{2,1,0:T(8,128)(2,1)} %w_hbm.1, s32[1,8,256]{2,1,0:T(8,128)} %p_ref.1), custom_call_target="tpu_custom_call" | custom-call | tf_op jit(solution)/shard_map/pallas_call | solution.py:361
  220.1 2.1 copy.4

commit v4 on v3

v4 whole, which is shorter than its diff:
```python
import functools
import math

import jax
import jax.numpy as jnp
from jax import lax
from jax.experimental import pallas as pl
from jax.experimental.pallas import tpu as pltpu
from jax.sharding import PartitionSpec as P

D = 3072
N = 256
H = N // 2
F = D // 2
MESH = pl.DeviceIdType.MESH
NEAR, Z0, Z1, Z2, X0, X1, Y0, Y1 = range(8)


def layout(counts):
    at, out = 0, {}
    for name, count in counts:
        out[name] = at
        at += count
    return out, at


T = 256
TILES = F // T

SEM, N_SEM = layout([
    ("near_raw", 1), ("in", 16), ("z_raw", 2), ("z_fwd", 16), ("perm", 10),
    ("z1", 12), ("z2", 12), ("z3", 6), ("z4", 6), ("x1", 12), ("x2", 6), ("y1", 6), ("y2", 6), ("y3", 6), ("out", 4), ("away", 8),
    ("cost", 12 * 2),
])


def kernel(w_hbm, p_ref, o_ref, perms, raw, first, cur, got, relay, relay_half, mine_g, near_g, mix, ssem, rsem, lsem):
    rep, h = lax.axis_index("rep"), lax.axis_index("slab")
    g = rep % 2
    far = 1 - h

    def flip(bit):
        return rep + (1 << bit) * (1 - 2 * ((rep // (1 << bit)) % 2))

    def core(base, c):
        return base - g + c

    def xor(a, b):
        return a + b - 2 * a * b

    near = (flip(0), h)
    chip = [flip(b) for b in range(8)]
    same = [(chip[b], h) for b in range(8)]

    wv = w_hbm.at[0]

    z, x = (rep // 2) % 8, (rep // 16) % 4
    z_next, z_last = (rep + 2 * ((z + 1) % 8 - z), h), (rep + 2 * ((z + 7) % 8 - z), h)
    x_next, x_last = (rep + 16 * ((x + 1) % 4 - x), h), (rep + 16 * ((x + 3) % 4 - x), h)

    y = (rep // 64) % 4
    inner = ((y + 1) // 2) % 2
    y_cross = (rep + 64 * (3 - 2 * y), h)
    peers = [near, z_next, z_last, x_next, x_last, same[Y0], y_cross]
    for c in range(2):
        peers.append((core(rep, c), far))
        peers.append((core(chip[Y1], c), far))
        for b in (Z0, Z2, X1, Y1):
            peers.append((core(chip[b], c), h))
    barrier = pltpu.get_barrier_semaphore()
    for peer in peers:
        pl.semaphore_signal(barrier, inc=1, device_id=peer, device_id_type=MESH)
    pl.semaphore_wait(barrier, len(peers))

    sent = []

    def send(src, dst, sem, device):
        copy = pltpu.make_async_remote_copy(
            src_ref=src, dst_ref=dst, send_sem=ssem.at[sem], recv_sem=rsem.at[sem],
            device_id=device, device_id_type=MESH,
        )
        copy.start()
        sent.append(copy)

    def arrived(dst, sem):
        pltpu.make_async_remote_copy(
            src_ref=dst, dst_ref=dst, send_sem=ssem.at[0], recv_sem=rsem.at[sem],
            device_id=near, device_id_type=MESH,
        ).wait_recv()

    def half(c):
        return pl.ds(c * F, F)

    slot, far_slot = xor(g, h), xor(g, far)
    my_rows, far_rows = h * H, far * H
    step = H // 8

    keep = pltpu.make_async_copy(
        wv.at[:, pl.ds(pl.multiple_of(g * F, F), F)],
        raw.at[0, slot, pl.ds(pl.multiple_of(my_rows, H), H)], lsem.at[1])
    keep.start()

    def send_in(q, c):
        src = wv.at[pl.ds(q * step, step), half(c)]
        dst = raw.at[0, far_slot, pl.ds(pl.multiple_of(my_rows + q * step, step), step)]
        copy = pltpu.make_async_remote_copy(
            src_ref=src, dst_ref=dst, send_sem=ssem.at[SEM["in"] + q * 2 + c],
            recv_sem=rsem.at[SEM["in"] + q * 2 + far_slot],
            device_id=(core(rep, c), far), device_id_type=MESH)
        copy.start()
        sent.append(copy)

    for q in range(8):
        for c in range(2):
            send_in(q, c)
    for c in range(2):
        copy = pltpu.make_async_remote_copy(
            src_ref=wv.at[:, half(c)],
            dst_ref=raw.at[1, slot, pl.ds(pl.multiple_of(my_rows, H), H)],
            send_sem=ssem.at[SEM["z_raw"] + c], recv_sem=rsem.at[SEM["z_raw"] + slot],
            device_id=(core(chip[Z0], c), h), device_id_type=MESH)
        copy.start()
        sent.append(copy)
    send(wv.at[:, pl.ds(pl.multiple_of((1 - g) * F, F), F)],
         raw.at[0, slot, pl.ds(pl.multiple_of(my_rows, H), H)], SEM["near_raw"], near)

    perms[0, slot] = p_ref[0]
    perm_to = [(0, near, 0)]
    for at, b in ((1, Z0), (2, Z2), (3, X1), (4, Y1)):
        for c in range(2):
            perm_to.append((at, (core(chip[b], c), h), c))
    for at, device, c in perm_to:
        copy = pltpu.make_async_remote_copy(
            src_ref=p_ref.at[0], dst_ref=perms.at[at, slot],
            send_sem=ssem.at[SEM["perm"] + at * 2 + c], recv_sem=rsem.at[SEM["perm"] + at * 2 + slot],
            device_id=device, device_id_type=MESH)
        copy.start()
        sent.append(copy)

    for q in range(8):
        for s in range(2):
            rows = pl.ds(pl.multiple_of(far_rows + q * step, step), step)
            arrived(raw.at[0, s, rows], SEM["in"] + q * 2 + s)
            send(raw.at[0, s, rows], raw.at[1, s, rows], SEM["z_fwd"] + q * 2 + s, same[Z0])

    keep.wait()
    arrived(raw.at[0, 1 - slot, pl.ds(pl.multiple_of(my_rows, H), H)], SEM["near_raw"])
    arrived(perms.at[0, 1 - slot], SEM["perm"] + (1 - slot))
    for at in range(1, 5):
        for s in range(2):
            arrived(perms.at[at, s], SEM["perm"] + at * 2 + s)

    def tile(t):
        return pl.ds(t * T, T)

    def cost_of(level, part, own, early=(), late=tuple(range(TILES)), wait=lambda t: None):
        def over(tiles, rows):
            return sum(lax.dot_general(
                part[rows, tile(t)], own[:, tile(t)], (((1,), (1,)), ((), ())), preferred_element_type=jnp.float32)
                for t in tiles)

        if early:
            for t in early:
                wait(t)
            mine_g[level] = over(early, slice(None))
        for t in late:
            wait(t)
        for q in range(2):
            rows = pl.ds(q * H, H)
            value = over(late, rows)
            mine_g[level, rows] = mine_g[level, rows] + value if early else value
            send(mine_g.at[level, rows], near_g.at[level, rows], SEM["cost"] + level * 2 + q, near)

    def fourth_of(level):
        for q in range(2):
            arrived(near_g.at[level, pl.ds(q * H, H)], SEM["cost"] + level * 2 + q)
        cost = (mine_g[level] + near_g[level]) * (1.0 / math.sqrt(D))
        squared = cost * cost
        return squared * squared

    def onehot_of(perm_row):
        neuron = lax.broadcasted_iota(jnp.int32, (N, N), 0)
        return jnp.where(neuron == perm_row, 0.5, 0.0)

    def mixing_of(fourth, perm_row):
        scale = 0.5 / (1.0 + jnp.sum(fourth, axis=0, keepdims=True))
        mix[0] = (onehot_of(perm_row) + fourth * scale).T.astype(jnp.bfloat16)

    def mix_tile(at, t, part, own, out):
        aligned = jnp.dot(mix[at], part[:, tile(t)], preferred_element_type=jnp.float32)
        out[:, tile(t)] = (
            (own[:, tile(t)].astype(jnp.float32) + aligned) * (1.0 / math.sqrt(2.0))).astype(jnp.bfloat16)

    def merge(level, perm_row, part, own, out, then=lambda t: None):
        mixing_of(fourth_of(level), perm_row)
        for t in range(TILES):
            mix_tile(0, t, part, own, out)
            then(t)

    def perm_of(at, r):
        return perms[at, 0, r:r + 1]

    cost_of(0, raw.at[0, 1], raw.at[0, 0])
    merge(0, perm_of(0, 0), raw.at[0, 1], raw.at[0, 0], first.at[0])
    for s in range(2):
        arrived(raw.at[1, s, pl.ds(pl.multiple_of(my_rows, H), H)], SEM["z_raw"] + s)
    for q in range(8):
        for s in range(2):
            rows = pl.ds(pl.multiple_of(far_rows + q * step, step), step)
            arrived(raw.at[1, s, rows], SEM["z_fwd"] + q * 2 + s)
    cost_of(1, raw.at[1, 1], raw.at[1, 0])
    merge(1, perm_of(1, 0), raw.at[1, 1], raw.at[1, 0], first.at[1])
    cost_of(2, first.at[1], first.at[0])

    L = TILES // 2
    EARLY = tuple(t for e in range(L - 1) for t in (e, e + L))
    LATE = (L - 1, 2 * L - 1)

    def quad(level, at, r, own, slots, wait_rings, wait_opposite, tmp, early, late):
        for t in range(TILES):
            wait_rings(t)
        cost_of(level, slots.at[0], own)
        merge(level, perm_of(0, r), slots.at[0], own, tmp.at[0])
        cost_of(level + 1, slots.at[2], slots.at[1], early, late, wait_opposite)
        merge(level + 1, perm_of(at, r), slots.at[2], slots.at[1], tmp.at[1])
        cost_of(level + 2, tmp.at[1], tmp.at[0])

    zq = got.at[pl.ds(0, 3)]

    def bit1(v):
        return (v // 2) % 2

    to_next, to_last = 2 * (1 - bit1((z + 1) % 8)), 2 * bit1((z + 7) % 8)
    from_last, from_next = 2 * (1 - bit1(z)), 2 * bit1(z)

    def send_z1(t):
        send(cur.at[0, :, tile(t)], relay.at[0, :, tile(t)], SEM["z1"] + t, z_next)
        send(cur.at[0, :, tile(t)], relay.at[1, :, tile(t)], SEM["z1"] + TILES + t, z_last)

    merge(2, perm_of(0, 1), first.at[1], first.at[0], cur.at[0], send_z1)
    for t in range(TILES):
        arrived(relay.at[0, :, tile(t)], SEM["z1"] + t)
        send(relay.at[0, :, tile(t)], zq.at[to_next, :, tile(t)], SEM["z2"] + t, z_next)
        arrived(relay.at[1, :, tile(t)], SEM["z1"] + TILES + t)
        send(relay.at[1, :, tile(t)], zq.at[to_last, :, tile(t)], SEM["z2"] + TILES + t, z_last)

    def rings_z(t):
        arrived(zq.at[from_last, :, tile(t)], SEM["z2"] + t)
        if t < L:
            send(zq.at[from_last, :, tile(t)], relay_half.at[0, :, tile(t)], SEM["z3"] + t, z_next)
        arrived(zq.at[from_next, :, tile(t)], SEM["z2"] + TILES + t)
        if t >= L:
            send(zq.at[from_next, :, tile(t)], relay_half.at[1, :, tile(t - L)], SEM["z3"] + t, z_last)

    def pass_on_z(t):
        side, there = (0, z_next) if t < L else (1, z_last)
        arrived(relay_half.at[side, :, tile(t % L)], SEM["z3"] + t)
        send(relay_half.at[side, :, tile(t % L)], zq.at[1, :, tile(t)], SEM["z4"] + t, there)

    def opposite_z(t):
        if t == 0:
            for e in EARLY + LATE:
                pass_on_z(e)
        arrived(zq.at[1, :, tile(t)], SEM["z4"] + t)

    def send_x1(t):
        send(cur.at[1, :, tile(t)], xq.at[2 * (x % 2), :, tile(t)], SEM["x1"] + t, x_next)
        send(cur.at[1, :, tile(t)], xq.at[2 * (1 - x % 2), :, tile(t)], SEM["x1"] + TILES + t, x_last)

    quad(3, 2, 2, cur.at[0], zq, rings_z, opposite_z, first.at[pl.ds(2, 2)], EARLY, LATE)

    xq = got.at[pl.ds(3, 3)]
    merge(5, perm_of(0, 3), first.at[3], first.at[2], cur.at[1], send_x1)

    def rings_x(t):
        arrived(xq.at[2 * (1 - x % 2), :, tile(t)], SEM["x1"] + t)
        if t < L:
            send(xq.at[2 * (1 - x % 2), :, tile(t)], xq.at[1, :, tile(t)], SEM["x2"] + t, x_next)
        arrived(xq.at[2 * (x % 2), :, tile(t)], SEM["x1"] + TILES + t)
        if t >= L:
            send(xq.at[2 * (x % 2), :, tile(t)], xq.at[1, :, tile(t)], SEM["x2"] + t, x_last)

    def opposite_x(t):
        arrived(xq.at[1, :, tile(t)], SEM["x2"] + t)

    quad(6, 3, 4, cur.at[1], xq, rings_x, opposite_x, first.at[pl.ds(4, 2)], EARLY, LATE)

    yq = got.at[pl.ds(6, 3)]

    def out_cols(c, s):
        return pl.ds(pl.multiple_of(c * F + s * (F // 2), F // 2), F // 2)

    @pl.when(inner == 0)
    def _():
        before = len(sent)

        def send_y1(t):
            send(cur.at[2, :, tile(t)], yq.at[0, :, tile(t)], SEM["y1"] + t, same[Y0])

        merge(8, perm_of(0, 5), first.at[5], first.at[4], cur.at[2], send_y1)
        for c in range(2):
            for s in range(2):
                arrived(o_ref.at[0, :, out_cols(c, s)], SEM["out"] + 2 * c + s)
        for copy in sent[before:]:
            copy.wait_send()
        del sent[before:]

    @pl.when(inner == 1)
    def _():
        before = len(sent)

        def send_y2(t):
            send(cur.at[2, :, tile(t)], yq.at[2, :, tile(t)], SEM["y2"] + t, y_cross)

        merge(8, perm_of(0, 5), first.at[5], first.at[4], cur.at[2], send_y2)

        def rings_y(t):
            arrived(yq.at[0, :, tile(t)], SEM["y1"] + t)
            send(yq.at[0, :, tile(t)], yq.at[1, :, tile(t)], SEM["y3"] + t, y_cross)

        def opposite_y(t):
            if t == 0:
                for e in range(TILES):
                    arrived(yq.at[2, :, tile(e)], SEM["y2"] + e)
            arrived(yq.at[1, :, tile(t)], SEM["y3"] + t)

        quad(9, 4, 6, cur.at[2], yq, rings_y, opposite_y, first.at[pl.ds(6, 2)],
             tuple(range(TILES - 1)), (TILES - 1,))
        ours, theirs = first.at[6], first.at[7]

        def away(src, rows, s, at, device):
            copy = pltpu.make_async_remote_copy(
                src_ref=src.at[pl.ds(pl.multiple_of(rows, H), H), pl.ds(s * (F // 2), F // 2)],
                dst_ref=o_ref.at[0, :, out_cols(g, s)],
                send_sem=ssem.at[SEM["away"] + 2 * at + s], recv_sem=rsem.at[SEM["out"] + 2 * g + s],
                device_id=device, device_id_type=MESH)
            copy.start()
            return copy

        fourth = fourth_of(11)
        mixing_of(fourth, perm_of(0, 7))
        scale = 0.5 / (1.0 + jnp.sum(fourth, axis=1, keepdims=True))
        mix[1] = (onehot_of(perm_of(4, 7)).T + fourth * scale).astype(jnp.bfloat16)
        leaving = []
        for s in range(2):
            for t in range(s * L, (s + 1) * L):
                mix_tile(1, t, ours, theirs, cur.at[4])
            leaving.append(away(cur.at[4], my_rows, s, 1, (core(chip[Y1], h), h)))
            leaving.append(away(cur.at[4], far_rows, s, 2, (core(chip[Y1], h), far)))
            for t in range(s * L, (s + 1) * L):
                mix_tile(0, t, theirs, ours, cur.at[3])
            leaving.append(away(cur.at[3], far_rows, s, 0, (core(rep, h), far)))

        @pl.when(slot == 0)
        def _():
            home = pltpu.make_async_copy(
                cur.at[3, pl.ds(pl.multiple_of(my_rows, H), H)],
                o_ref.at[0, :, pl.ds(pl.multiple_of(g * F, F), F)], lsem.at[2])
            home.start()
            home.wait()
            for s in range(2):
                arrived(o_ref.at[0, :, out_cols(1 - g, s)], SEM["out"] + 2 * (1 - g) + s)

        @pl.when(slot == 1)
        def _():
            home = [away(cur.at[3], my_rows, s, 3, near) for s in range(2)]
            for c in range(2):
                for s in range(2):
                    arrived(o_ref.at[0, :, out_cols(c, s)], SEM["out"] + 2 * c + s)
            for copy in home:
                copy.wait_send()

        for copy in leaving + sent[before:]:
            copy.wait_send()
        del sent[before:]

    for copy in sent:
        copy.wait_send()


def local(weights, perms):
    rows = (N, F)
    return pl.pallas_call(
        kernel,
        out_shape=jax.ShapeDtypeStruct((1, H, D), jnp.bfloat16),
        in_specs=[pl.BlockSpec(memory_space=pltpu.HBM), pl.BlockSpec(memory_space=pltpu.VMEM)],
        out_specs=pl.BlockSpec(memory_space=pl.ANY),
        scratch_shapes=[
            pltpu.VMEM((5, 2, 8, N), jnp.int32),
            pltpu.VMEM((2, 2, *rows), jnp.bfloat16),
            pltpu.VMEM((8, *rows), jnp.bfloat16),
            pltpu.VMEM((5, *rows), jnp.bfloat16),
            pltpu.VMEM((9, *rows), jnp.bfloat16),
            pltpu.VMEM((2, *rows), jnp.bfloat16),
            pltpu.VMEM((2, N, F // 2), jnp.bfloat16),
            pltpu.VMEM((12, N, N), jnp.float32),
            pltpu.VMEM((12, N, N), jnp.float32),
            pltpu.VMEM((2, N, N), jnp.bfloat16),
            pltpu.SemaphoreType.DMA((N_SEM,)),
            pltpu.SemaphoreType.DMA((N_SEM,)),
            pltpu.SemaphoreType.DMA((3,)),
        ],
        compiler_params=pltpu.CompilerParams(
            collective_id=0, has_side_effects=True, vmem_limit_bytes=40 * 1024 * 1024),
    )(weights, perms)


def solution(mesh):
    placed = (P("rep", "slab", None), P("rep", None, None))
    return jax.shard_map(
        local, mesh=mesh, in_specs=placed, out_specs=P("rep", "slab", None), check_vma=False
    )
```

time: 222 us -> 223 us (level)
  the two profiles are of different devices: /device:TPU:1 before, /device:TPU:9 now
where the time goes in v4:
time: 223 us
  Pallas kernels  220 us (99%)
  local copies, waits for them, and re-layouts  2.71 us (1%)
    pallas_call x1, Pallas kernels, local(): pl.pallas_call(kernel, out_shape=jax.ShapeDtypeStruct((1, H, D), jnp.bflo...  220 us

profile of v4, /device:TPU:9, one launch (start us, length us, event | category | flops | bytes accessed | tf_op | source)
XLA Modules:
  0.0 222.8 jit_solution(10043311337625264992)
XLA Ops:
  0.0 0.0 copy-start
  0.0 1.1 copy-done
  1.1 0.0 copy-start.1
  1.1 0.7 copy-done.1
  1.8 220.1 %shard_map.28 = bf16[1,128,3072]{2,1,0:T(8,128)(2,1)S(1)} custom-call(bf16[1,128,3072]{2,1,0:T(8,128)(2,1)S(1)} %copy-done, s32[1,8,256]{2,1,0:T(8,128)S(1)} %copy-done.1), custom_call_target="tpu_custom_call" | custom-call | tf_op jit(solution)/shard_map/pallas_call | solution.py:383
  221.9 0.9 copy.4
Async XLA Ops:
  0.0 1.1 copy-start
  1.1 0.7 copy-start.1

commit v5 on v3

--- a/solution.py
+++ b/solution.py
@@ -27,11 +27,11 @@
 SEM, N_SEM = layout([
     ("near_raw", 1), ("in", 16), ("z_raw", 2), ("z_fwd", 16), ("perm", 10),
     ("z1", 8), ("z2", 8), ("z3", 4), ("z4", 4), ("x1", 8), ("x2", 4), ("y1", 4), ("y2", 4), ("y3", 4), ("out", 2), ("away", 4),
-    ("cost", 12 * 4),
+    ("cost", 6 * 4), ("pair", 3 * 4), ("seen", 3),
 ])
 
 
-def kernel(w_hbm, p_ref, o_ref, wv, perms, raw, first, cur, got, relay, relay_half, mine_g, near_g, mix, ssem, rsem, lsem):
+def kernel(w_hbm, p_ref, o_ref, wv, perms, raw, first, cur, got, relay, relay_half, mine_g, near_g, mine_p, near_p, mine_e, near_e, seen, next_fourth, onehot, mix, ssem, rsem, lsem):
     rep, h = lax.axis_index("rep"), lax.axis_index("slab")
     g = rep % 2
     far = 1 - h
@@ -177,20 +177,27 @@
 
     def mixing_of(fourth, perm_row):
         scale = 0.5 / (1.0 + jnp.sum(fourth, axis=0, keepdims=True))
-        mix[...] = (onehot_of(perm_row) + fourth * scale).T.astype(jnp.bfloat16)
-
-    def mix_in(part, own, out, then):
+        mix[0] = (onehot_of(perm_row) + fourth * scale).T.astype(jnp.bfloat16)
+
+    def rows2(q):
+        return pl.ds(q * H, H)
+
+    def mix_rows(at, rows, part, own, out):
         for t in range(F // N):
             tile = pl.ds(t * N, N)
-            aligned = jnp.dot(mix[...], part[:, tile], preferred_element_type=jnp.float32)
-            out[:, tile] = (
-                (own[:, tile].astype(jnp.float32) + aligned) * (1.0 / math.sqrt(2.0))).astype(jnp.bfloat16)
-        for q in range(4):
-            then(q)
+            aligned = jnp.dot(mix[at, rows], part[:, tile], preferred_element_type=jnp.float32)
+            out[rows, tile] = (
+                (own[rows, tile].astype(jnp.float32) + aligned) * (1.0 / math.sqrt(2.0))).astype(jnp.bfloat16)
+
+    def merge_with(fourth, perm_row, part, own, out, then=lambda q: None):
+        mixing_of(fourth, perm_row)
+        for q in range(2):
+            mix_rows(0, rows2(q), part, own, out)
+            then(2 * q)
+            then(2 * q + 1)
 
     def merge(level, perm_row, part, own, out, then=lambda q: None):
-        mixing_of(fourth_of(level), perm_row)
-        mix_in(part, own, out, then)
+        merge_with(fourth_of(level), perm_row, part, own, out, then)
 
     def perm_of(at, r):
         return perms[at, 0, r:r + 1]
@@ -207,15 +214,51 @@
     merge(1, perm_of(1, 0), raw.at[1, 1], raw.at[1, 0], first.at[1])
     cost_part(2, 0, first.at[1], first.at[0], 1)
 
-    def quad(level, at, r, own, slots, wait_rings, wait_last, tmp):
+    def quad(k, at, r, own, slots, wait_rings, order, wait_opposite, tmp):
+        level = 3 + k
         for q in range(4):
             wait_rings(q)
             cost_part(level, q, slots.at[0], own)
+        onehot[...] = onehot_of(perm_of(at, r)).T
         merge(level, perm_of(0, r), slots.at[0], own, tmp.at[0])
-        wait_last()
-        cost_part(level + 1, 0, slots.at[2], slots.at[1], 1)
-        merge(level + 1, perm_of(at, r), slots.at[2], slots.at[1], tmp.at[1])
-        cost_part(level + 2, 0, tmp.at[1], tmp.at[0], 1)
+        mine_e[k] = lax.dot_general(
+            slots[2], tmp[0], (((1,), (1,)), ((), ())), preferred_element_type=jnp.float32)
+        send(mine_e.at[k], near_e.at[k], SEM["seen"] + k, near)
+
+        def sums(q):
+            mine_p[k, rows4(q), pl.ds(0, N)] = lax.dot_general(
+                slots[1, rows4(q)], slots[2], (((1,), (1,)), ((), ())), preferred_element_type=jnp.float32)
+            mine_p[k, rows4(q), pl.ds(N, N)] = lax.dot_general(
+                slots[1, rows4(q)], tmp[0], (((1,), (1,)), ((), ())), preferred_element_type=jnp.float32)
+            send(mine_p.at[k, rows4(q)], near_p.at[k, rows4(q)], SEM["pair"] + 4 * k + q, near)
+
+        def level_of(q):
+            rows = rows4(q)
+            arrived(near_p.at[k, rows], SEM["pair"] + 4 * k + q)
+            cost = (mine_p[k, rows, pl.ds(0, N)] + near_p[k, rows, pl.ds(0, N)]) * (1.0 / math.sqrt(D))
+            squared = cost * cost
+            fourth = squared * squared
+            mixing = (onehot[rows] + fourth * (0.5 / (1.0 + jnp.sum(fourth, axis=1, keepdims=True)))).astype(jnp.bfloat16)
+            mix[1, rows] = mixing
+            through = (jnp.dot(mixing, seen[0], preferred_element_type=jnp.float32)
+                       + jnp.dot(mixing, seen[1], preferred_element_type=jnp.float32))
+            direct = mine_p[k, rows, pl.ds(N, N)] + near_p[k, rows, pl.ds(N, N)]
+            cost = (direct + through) * (1.0 / math.sqrt(2.0 * D))
+            squared = cost * cost
+            next_fourth[rows] = squared * squared
+            mix_rows(1, rows, slots.at[2], slots.at[1], tmp.at[1])
+
+        for e, q in enumerate(order):
+            wait_opposite(q)
+            sums(q)
+            if e == 0:
+                arrived(near_e.at[k], SEM["seen"] + k)
+                both = mine_e[k] + near_e[k]
+                seen[0] = both.astype(jnp.bfloat16)
+                seen[1] = (both - seen[0].astype(jnp.float32)).astype(jnp.bfloat16)
+            else:
+                level_of(order[e - 1])
+        level_of(order[-1])
 
     zq = got.at[pl.ds(0, 3)]
 
@@ -244,22 +287,21 @@
         if q >= 2:
             send(zq.at[from_next, rows4(q)], relay_half.at[1, rows4(q - 2)], SEM["z3"] + q, z_last)
 
-    def last_z():
-        for q in range(2):
-            arrived(relay_half.at[0, rows4(q)], SEM["z3"] + q)
-            send(relay_half.at[0, rows4(q)], zq.at[1, rows4(q)], SEM["z4"] + q, z_next)
-            arrived(relay_half.at[1, rows4(q)], SEM["z3"] + 2 + q)
-            send(relay_half.at[1, rows4(q)], zq.at[1, rows4(q + 2)], SEM["z4"] + 2 + q, z_last)
-        for q in range(4):
-            arrived(zq.at[1, rows4(q)], SEM["z4"] + q)
+    def opposite_z(q):
+        if q == 0:
+            for e in (0, 2, 1, 3):
+                side, there = (0, z_next) if e < 2 else (1, z_last)
+                arrived(relay_half.at[side, rows4(e % 2)], SEM["z3"] + e)
+                send(relay_half.at[side, rows4(e % 2)], zq.at[1, rows4(e)], SEM["z4"] + e, there)
+        arrived(zq.at[1, rows4(q)], SEM["z4"] + q)
 
     def send_x1(q):
         send(cur.at[1, rows4(q)], xq.at[2 * (x % 2), rows4(q)], SEM["x1"] + q, x_next)
         send(cur.at[1, rows4(q)], xq.at[2 * (1 - x % 2), rows4(q)], SEM["x1"] + 4 + q, x_last)
 
     xq = got.at[pl.ds(3, 3)]
-    quad(3, 2, 2, cur.at[0], zq, rings_z, last_z, first.at[pl.ds(2, 2)])
-    merge(5, perm_of(0, 3), first.at[3], first.at[2], cur.at[1], send_x1)
+    quad(0, 2, 2, cur.at[0], zq, rings_z, (0, 2, 1, 3), opposite_z, first.at[pl.ds(2, 2)])
+    merge_with(next_fourth[...], perm_of(0, 3), first.at[3], first.at[2], cur.at[1], send_x1)
 
     def rings_x(q):
         arrived(xq.at[2 * (1 - x % 2), rows4(q)], SEM["x1"] + q)
@@ -269,11 +311,10 @@
         if q >= 2:
             send(xq.at[2 * (x % 2), rows4(q)], xq.at[1, rows4(q)], SEM["x2"] + q, x_last)
 
-    def last_x():
-        for q in range(4):
-            arrived(xq.at[1, rows4(q)], SEM["x2"] + q)
-
-    quad(6, 3, 4, cur.at[1], xq, rings_x, last_x, first.at[pl.ds(4, 2)])
+    def opposite_x(q):
+        arrived(xq.at[1, rows4(q)], SEM["x2"] + q)
+
+    quad(1, 3, 4, cur.at[1], xq, rings_x, (0, 2, 1, 3), opposite_x, first.at[pl.ds(4, 2)])
 
     yq = got.at[pl.ds(6, 3)]
     o_cols = pl.ds(pl.multiple_of(g * F, F), F)
@@ -281,13 +322,14 @@
     @pl.when(inner == 0)
     def _():
         outer_sends = []
-        merge(8, perm_of(0, 5), first.at[5], first.at[4], cur.at[2])
-        for q in range(4):
+        def send_y1(q):
             copy = pltpu.make_async_remote_copy(
                 src_ref=cur.at[2, rows4(q)], dst_ref=yq.at[0, rows4(q)], send_sem=ssem.at[SEM["y1"] + q],
                 recv_sem=rsem.at[SEM["y1"] + q], device_id=same[Y0], device_id_type=MESH)
             copy.start()
             outer_sends.append(copy)
+
+        merge_with(next_fourth[...], perm_of(0, 5), first.at[5], first.at[4], cur.at[2], send_y1)
         for c in range(2):
             arrived(o_ref.at[0, :, half(c)], SEM["out"] + c)
         for copy in outer_sends:
@@ -300,19 +342,17 @@
         def send_y2(q):
             send(cur.at[2, rows4(q)], yq.at[2, rows4(q)], SEM["y2"] + q, y_cross)
 
-        merge(8, perm_of(0, 5), first.at[5], first.at[4], cur.at[2], send_y2)
+        merge_with(next_fourth[...], perm_of(0, 5), first.at[5], first.at[4], cur.at[2], send_y2)
 
         def rings_y(q):
             arrived(yq.at[0, rows4(q)], SEM["y1"] + q)
             send(yq.at[0, rows4(q)], yq.at[1, rows4(q)], SEM["y3"] + q, y_cross)
-
-        def last_y():
-            for q in range(4):
-                arrived(yq.at[2, rows4(q)], SEM["y2"] + q)
-            for q in range(4):
-                arrived(yq.at[1, rows4(q)], SEM["y3"] + q)
-
-        quad(9, 4, 6, cur.at[2], yq, rings_y, last_y, first.at[pl.ds(6, 2)])
+            arrived(yq.at[2, rows4(q)], SEM["y2"] + q)
+
+        def opposite_y(q):
+            arrived(yq.at[1, rows4(q)], SEM["y3"] + q)
+
+        quad(2, 4, 6, cur.at[2], yq, rings_y, (0, 1, 2, 3), opposite_y, first.at[pl.ds(6, 2)])
         ours, theirs = first.at[6], first.at[7]
 
         def away(src, rows, at, device):
@@ -323,15 +363,19 @@
             copy.start()
             return copy
 
-        fourth = fourth_of(11)
+        fourth = next_fourth[...]
         mixing_of(fourth, perm_of(0, 7))
-        mix_in(theirs, ours, cur.at[3], lambda q: None)
-        leaving = [away(cur.at[3], far_rows, 0, (core(rep, h), far))]
         scale = 0.5 / (1.0 + jnp.sum(fourth, axis=1, keepdims=True))
-        mix[...] = (onehot_of(perm_of(4, 7)).T + fourth * scale).astype(jnp.bfloat16)
-        mix_in(ours, theirs, cur.at[4], lambda q: None)
+        mix[1] = (onehot_of(perm_of(4, 7)).T + fourth * scale).astype(jnp.bfloat16)
+        leaving = []
+        far_half, my_half = pl.ds(pl.multiple_of(far_rows, H), H), pl.ds(pl.multiple_of(my_rows, H), H)
+        mix_rows(1, far_half, ours, theirs, cur.at[4])
+        leaving.append(away(cur.at[4], far_rows, 2, (core(chip[Y1], h), far)))
+        mix_rows(0, far_half, theirs, ours, cur.at[3])
+        leaving.append(away(cur.at[3], far_rows, 0, (core(rep, h), far)))
+        mix_rows(1, my_half, ours, theirs, cur.at[4])
         leaving.append(away(cur.at[4], my_rows, 1, (core(chip[Y1], h), h)))
-        leaving.append(away(cur.at[4], far_rows, 2, (core(chip[Y1], h), far)))
+        mix_rows(0, my_half, theirs, ours, cur.at[3])
 
         @pl.when(slot == 0)
         def _():
@@ -372,9 +416,16 @@
             pltpu.VMEM((9, *rows), jnp.bfloat16),
             pltpu.VMEM((2, *rows), jnp.bfloat16),
             pltpu.VMEM((2, H, F), jnp.bfloat16),
-            pltpu.VMEM((12, N, N), jnp.float32),
-            pltpu.VMEM((12, N, N), jnp.float32),
-            pltpu.VMEM((N, N), jnp.bfloat16),
+            pltpu.VMEM((6, N, N), jnp.float32),
+            pltpu.VMEM((6, N, N), jnp.float32),
+            pltpu.VMEM((3, N, 2 * N), jnp.float32),
+            pltpu.VMEM((3, N, 2 * N), jnp.float32),
+            pltpu.VMEM((3, N, N), jnp.float32),
+            pltpu.VMEM((3, N, N), jnp.float32),
+            pltpu.VMEM((2, N, N), jnp.bfloat16),
+            pltpu.VMEM((N, N), jnp.float32),
+            pltpu.VMEM((N, N), jnp.float32),
+            pltpu.VMEM((2, N, N), jnp.bfloat16),
             pltpu.SemaphoreType.DMA((N_SEM,)),
             pltpu.SemaphoreType.DMA((N_SEM,)),
             pltpu.SemaphoreType.DMA((3,)),

time: 222 us -> 220 us (level)
  the two profiles are of different devices: /device:TPU:1 before, /device:TPU:9 now
where the time goes in v5:
time: 220 us; the launch traced here: 219 us
  Pallas kernels  217 us (99%)
    pallas_call x1, Pallas kernels, local(): pl.pallas_call(kernel, out_shape=jax.ShapeDtypeStruct((1, H, D), jnp.bflo...  217 us

profile of v5, /device:TPU:9, one launch (start us, length us, event | category | flops | bytes accessed | tf_op | source)
XLA Modules:
  0.0 219.5 jit_solution(10463592317816077779)
XLA Ops:
  0.0 217.4 %shard_map.28 = bf16[1,128,3072]{2,1,0:T(8,128)(2,1)} custom-call(bf16[1,128,3072]{2,1,0:T(8,128)(2,1)} %w_hbm.1, s32[1,8,256]{2,1,0:T(8,128)} %p_ref.1), custom_call_target="tpu_custom_call" | custom-call | tf_op jit(solution)/shard_map/pallas_call | solution.py:405
  217.4 2.1 copy.4

commit v6 on v5

--- a/solution.py
+++ b/solution.py
@@ -25,13 +25,13 @@
 
 
 SEM, N_SEM = layout([
-    ("near_raw", 1), ("in", 16), ("z_raw", 2), ("z_fwd", 16), ("perm", 10),
+    ("near_raw", 1), ("in", 32), ("z_raw", 2), ("z_fwd", 32), ("perm", 10),
     ("z1", 8), ("z2", 8), ("z3", 4), ("z4", 4), ("x1", 8), ("x2", 4), ("y1", 4), ("y2", 4), ("y3", 4), ("out", 2), ("away", 4),
     ("cost", 6 * 4), ("pair", 3 * 4), ("seen", 3),
 ])
 
 
-def kernel(w_hbm, p_ref, o_ref, wv, perms, raw, first, cur, got, relay, relay_half, mine_g, near_g, mine_p, near_p, mine_e, near_e, seen, next_fourth, onehot, mix, ssem, rsem, lsem):
+def kernel(w_hbm, p_hbm, o_ref, wv, perms, raw, first, cur, got, relay, relay_half, mine_g, near_g, mine_p, near_p, mine_e, near_e, seen, next_fourth, onehot, mix, ssem, rsem, lsem):
     rep, h = lax.axis_index("rep"), lax.axis_index("slab")
     g = rep % 2
     far = 1 - h
@@ -51,6 +51,9 @@
 
     load = pltpu.make_async_copy(w_hbm.at[0], wv, lsem.at[0])
     load.start()
+    slot = g + h - 2 * g * h
+    load_perms = pltpu.make_async_copy(p_hbm.at[0], perms.at[0, slot], lsem.at[3])
+    load_perms.start()
 
     z, x = (rep // 2) % 8, (rep // 16) % 4
     z_next, z_last = (rep + 2 * ((z + 1) % 8 - z), h), (rep + 2 * ((z + 7) % 8 - z), h)
@@ -89,7 +92,7 @@
     def half(c):
         return pl.ds(c * F, F)
 
-    slot, far_slot = xor(g, h), xor(g, far)
+    far_slot = xor(g, far)
     my_rows, far_rows = h * H, far * H
     step = H // 8
 
@@ -99,19 +102,23 @@
         raw.at[0, slot, pl.ds(pl.multiple_of(my_rows, H), H)], lsem.at[1])
     keep.start()
 
-    def send_in(q, c):
-        src = wv.at[pl.ds(q * step, step), half(c)]
-        dst = raw.at[0, far_slot, pl.ds(pl.multiple_of(my_rows + q * step, step), step)]
+    def piece(e):
+        return pl.ds(e * (F // 2), F // 2)
+
+    def send_in(q, e, c):
+        src = wv.at[pl.ds(q * step, step), pl.ds(c * F + e * (F // 2), F // 2)]
+        dst = raw.at[0, far_slot, pl.ds(pl.multiple_of(my_rows + q * step, step), step), piece(e)]
         copy = pltpu.make_async_remote_copy(
-            src_ref=src, dst_ref=dst, send_sem=ssem.at[SEM["in"] + q * 2 + c],
-            recv_sem=rsem.at[SEM["in"] + q * 2 + far_slot],
+            src_ref=src, dst_ref=dst, send_sem=ssem.at[SEM["in"] + q * 4 + e * 2 + c],
+            recv_sem=rsem.at[SEM["in"] + q * 4 + e * 2 + far_slot],
             device_id=(core(rep, c), far), device_id_type=MESH)
         copy.start()
         sent.append(copy)
 
     for q in range(8):
-        for c in range(2):
-            send_in(q, c)
+        for e in range(2):
+            for c in range(2):
+                send_in(q, e, c)
     for c in range(2):
         copy = pltpu.make_async_remote_copy(
             src_ref=wv.at[:, half(c)],
@@ -123,24 +130,26 @@
     send(wv.at[:, pl.ds(pl.multiple_of((1 - g) * F, F), F)],
          raw.at[0, slot, pl.ds(pl.multiple_of(my_rows, H), H)], SEM["near_raw"], near)
 
-    perms[0, slot] = p_ref[0]
+    load_perms.wait()
     perm_to = [(0, near, 0)]
     for at, b in ((1, Z0), (2, Z2), (3, X1), (4, Y1)):
         for c in range(2):
             perm_to.append((at, (core(chip[b], c), h), c))
     for at, device, c in perm_to:
         copy = pltpu.make_async_remote_copy(
-            src_ref=p_ref.at[0], dst_ref=perms.at[at, slot],
+            src_ref=perms.at[0, slot], dst_ref=perms.at[at, slot],
             send_sem=ssem.at[SEM["perm"] + at * 2 + c], recv_sem=rsem.at[SEM["perm"] + at * 2 + slot],
             device_id=device, device_id_type=MESH)
         copy.start()
         sent.append(copy)
 
     for q in range(8):
-        for s in range(2):
-            rows = pl.ds(pl.multiple_of(far_rows + q * step, step), step)
-            arrived(raw.at[0, s, rows], SEM["in"] + q * 2 + s)
-            send(raw.at[0, s, rows], raw.at[1, s, rows], SEM["z_fwd"] + q * 2 + s, same[Z0])
+        rows = pl.ds(pl.multiple_of(far_rows + q * step, step), step)
+        for e in range(2):
+            for s in range(2):
+                at = q * 4 + e * 2 + s
+                arrived(raw.at[0, s, rows, piece(e)], SEM["in"] + at)
+                send(raw.at[0, s, rows, piece(e)], raw.at[1, s, rows, piece(e)], SEM["z_fwd"] + at, same[Z0])
 
     keep.wait()
     arrived(raw.at[0, 1 - slot, pl.ds(pl.multiple_of(my_rows, H), H)], SEM["near_raw"])
@@ -191,10 +200,10 @@
 
     def merge_with(fourth, perm_row, part, own, out, then=lambda q: None):
         mixing_of(fourth, perm_row)
-        for q in range(2):
-            mix_rows(0, rows2(q), part, own, out)
-            then(2 * q)
-            then(2 * q + 1)
+        for first_piece, count in ((0, 1), (1, 1), (2, 2)):
+            mix_rows(0, pl.ds(first_piece * Q, count * Q), part, own, out)
+            for q in range(first_piece, first_piece + count):
+                then(q)
 
     def merge(level, perm_row, part, own, out, then=lambda q: None):
         merge_with(fourth_of(level), perm_row, part, own, out, then)
@@ -207,9 +216,10 @@
     for s in range(2):
         arrived(raw.at[1, s, pl.ds(pl.multiple_of(my_rows, H), H)], SEM["z_raw"] + s)
     for q in range(8):
-        for s in range(2):
-            rows = pl.ds(pl.multiple_of(far_rows + q * step, step), step)
-            arrived(raw.at[1, s, rows], SEM["z_fwd"] + q * 2 + s)
+        rows = pl.ds(pl.multiple_of(far_rows + q * step, step), step)
+        for e in range(2):
+            for s in range(2):
+                arrived(raw.at[1, s, rows, piece(e)], SEM["z_fwd"] + q * 4 + e * 2 + s)
     cost_part(1, 0, raw.at[1, 1], raw.at[1, 0], 1)
     merge(1, perm_of(1, 0), raw.at[1, 1], raw.at[1, 0], first.at[1])
     cost_part(2, 0, first.at[1], first.at[0], 1)
@@ -365,14 +375,14 @@
 
         fourth = next_fourth[...]
         mixing_of(fourth, perm_of(0, 7))
+        leaving = []
+        far_half, my_half = pl.ds(pl.multiple_of(far_rows, H), H), pl.ds(pl.multiple_of(my_rows, H), H)
+        mix_rows(0, far_half, theirs, ours, cur.at[3])
+        leaving.append(away(cur.at[3], far_rows, 0, (core(rep, h), far)))
         scale = 0.5 / (1.0 + jnp.sum(fourth, axis=1, keepdims=True))
         mix[1] = (onehot_of(perm_of(4, 7)).T + fourth * scale).astype(jnp.bfloat16)
-        leaving = []
-        far_half, my_half = pl.ds(pl.multiple_of(far_rows, H), H), pl.ds(pl.multiple_of(my_rows, H), H)
         mix_rows(1, far_half, ours, theirs, cur.at[4])
         leaving.append(away(cur.at[4], far_rows, 2, (core(chip[Y1], h), far)))
-        mix_rows(0, far_half, theirs, ours, cur.at[3])
-        leaving.append(away(cur.at[3], far_rows, 0, (core(rep, h), far)))
         mix_rows(1, my_half, ours, theirs, cur.at[4])
         leaving.append(away(cur.at[4], my_rows, 1, (core(chip[Y1], h), h)))
         mix_rows(0, my_half, theirs, ours, cur.at[3])
@@ -405,7 +415,7 @@
     return pl.pallas_call(
         kernel,
         out_shape=jax.ShapeDtypeStruct((1, H, D), jnp.bfloat16),
-        in_specs=[pl.BlockSpec(memory_space=pl.ANY), pl.BlockSpec(memory_space=pltpu.VMEM)],
+        in_specs=[pl.BlockSpec(memory_space=pl.ANY), pl.BlockSpec(memory_space=pl.ANY)],
         out_specs=pl.BlockSpec(memory_space=pl.ANY),
         scratch_shapes=[
             pltpu.VMEM((H, D), jnp.bfloat16),
@@ -428,7 +438,7 @@
             pltpu.VMEM((2, N, N), jnp.bfloat16),
             pltpu.SemaphoreType.DMA((N_SEM,)),
             pltpu.SemaphoreType.DMA((N_SEM,)),
-            pltpu.SemaphoreType.DMA((3,)),
+            pltpu.SemaphoreType.DMA((4,)),
         ],
         compiler_params=pltpu.CompilerParams(
             collective_id=0, has_side_effects=True, vmem_limit_bytes=60 * 1024 * 1024),

time: 220 us -> 222 us (level)
  the two profiles are of different devices: /device:TPU:9 before, /device:TPU:1 now
where the time goes in v6:
time: 222 us; the launch traced here: 221 us
  Pallas kernels  219 us (99%)
    pallas_call x1, Pallas kernels, local(): pl.pallas_call(kernel, out_shape=jax.ShapeDtypeStruct((1, H, D), jnp.bflo...  219 us

profile of v6, /device:TPU:1, one launch (start us, length us, event | category | flops | bytes accessed | tf_op | source)
XLA Modules:
  0.0 221.4 jit_solution(1584445287924557893)
XLA Ops:
  0.0 219.3 %shard_map.28 = bf16[1,128,3072]{2,1,0:T(8,128)(2,1)} custom-call(bf16[1,128,3072]{2,1,0:T(8,128)(2,1)} %w_hbm.1, s32[1,8,256]{2,1,0:T(8,128)} %p_hbm.1), custom_call_target="tpu_custom_call" | custom-call | tf_op jit(solution)/shard_map/pallas_call | solution.py:415
  219.3 2.1 copy.4

commit v7 on v6

--- a/solution.py
+++ b/solution.py
@@ -370,38 +370,49 @@
                 src_ref=src.at[pl.ds(pl.multiple_of(rows, H), H)], dst_ref=o_ref.at[0, :, o_cols],
                 send_sem=ssem.at[SEM["away"] + at], recv_sem=rsem.at[SEM["out"] + g],
                 device_id=device, device_id_type=MESH)
-            copy.start()
             return copy
 
         fourth = next_fourth[...]
         mixing_of(fourth, perm_of(0, 7))
-        leaving = []
         far_half, my_half = pl.ds(pl.multiple_of(far_rows, H), H), pl.ds(pl.multiple_of(my_rows, H), H)
+        ours_far = away(cur.at[3], far_rows, 0, (core(rep, h), far))
+        theirs_far = away(cur.at[4], far_rows, 2, (core(chip[Y1], h), far))
+        theirs_near = away(cur.at[4], my_rows, 1, (core(chip[Y1], h), h))
+        ours_near = away(cur.at[3], my_rows, 3, near)
         mix_rows(0, far_half, theirs, ours, cur.at[3])
-        leaving.append(away(cur.at[3], far_rows, 0, (core(rep, h), far)))
+        ours_far.start()
         scale = 0.5 / (1.0 + jnp.sum(fourth, axis=1, keepdims=True))
         mix[1] = (onehot_of(perm_of(4, 7)).T + fourth * scale).astype(jnp.bfloat16)
         mix_rows(1, far_half, ours, theirs, cur.at[4])
-        leaving.append(away(cur.at[4], far_rows, 2, (core(chip[Y1], h), far)))
-        mix_rows(1, my_half, ours, theirs, cur.at[4])
-        leaving.append(away(cur.at[4], my_rows, 1, (core(chip[Y1], h), h)))
+        theirs_far.start()
         mix_rows(0, my_half, theirs, ours, cur.at[3])
 
         @pl.when(slot == 0)
         def _():
-            home = pltpu.make_async_copy(
-                cur.at[3, pl.ds(pl.multiple_of(my_rows, H), H)], o_ref.at[0, :, o_cols], lsem.at[2])
+            home = pltpu.make_async_copy(cur.at[3, my_half], o_ref.at[0, :, o_cols], lsem.at[2])
             home.start()
             home.wait()
-            arrived(o_ref.at[0, :, pl.ds(pl.multiple_of((1 - g) * F, F), F)], SEM["out"] + 1 - g)
 
         @pl.when(slot == 1)
         def _():
-            home = away(cur.at[3], my_rows, 3, near)
+            ours_near.start()
+
+        mix_rows(1, my_half, ours, theirs, cur.at[4])
+        ours_far.wait_send()
+        theirs_far.wait_send()
+        theirs_near.start()
+
+        @pl.when(slot == 0)
+        def _():
+            arrived(o_ref.at[0, :, pl.ds(pl.multiple_of((1 - g) * F, F), F)], SEM["out"] + 1 - g)
+
+        @pl.when(slot == 1)
+        def _():
             for c in range(2):
                 arrived(o_ref.at[0, :, half(c)], SEM["out"] + c)
-            home.wait_send()
-
+            ours_near.wait_send()
+
+        leaving = [theirs_near]
         for copy in leaving + sent[before:]:
             copy.wait_send()
         del sent[before:]

time: 222 us -> 218 us (0.982)
  the two profiles are of different devices: /device:TPU:1 before, /device:TPU:57 now
where the time goes in v7:
time: 218 us
  Pallas kernels  216 us (99%)
    pallas_call x1, Pallas kernels, local(): pl.pallas_call(kernel, out_shape=jax.ShapeDtypeStruct((1, H, D), jnp.bflo...  216 us

profile of v7, /device:TPU:57, one launch (start us, length us, event | category | flops | bytes accessed | tf_op | source)
XLA Modules:
  0.0 218.2 jit_solution(16995018769725394161)
XLA Ops:
  0.0 216.1 %shard_map.28 = bf16[1,128,3072]{2,1,0:T(8,128)(2,1)} custom-call(bf16[1,128,3072]{2,1,0:T(8,128)(2,1)} %w_hbm.1, s32[1,8,256]{2,1,0:T(8,128)} %p_hbm.1), custom_call_target="tpu_custom_call" | custom-call | tf_op jit(solution)/shard_map/pallas_call | solution.py:426
  216.2 2.1 copy.4

commit v8 on v7

--- a/solution.py
+++ b/solution.py
@@ -425,7 +425,7 @@
     rows = (N, F)
     return pl.pallas_call(
         kernel,
-        out_shape=jax.ShapeDtypeStruct((1, H, D), jnp.bfloat16),
+        out_shape=pltpu.VMEM((1, H, D), jnp.bfloat16),
         in_specs=[pl.BlockSpec(memory_space=pl.ANY), pl.BlockSpec(memory_space=pl.ANY)],
         out_specs=pl.BlockSpec(memory_space=pl.ANY),
         scratch_shapes=[

time: 218 us -> 217 us (level)
  no operation moved by 1% of the time
where the time goes in v8:
time: 217 us
  Pallas kernels  216 us (100%)
    pallas_call x1, Pallas kernels, local(): pl.pallas_call(kernel, out_shape=pltpu.VMEM((1, H, D), jnp.bfloat16), in_...  216 us

profile of v8, /device:TPU:57, one launch (start us, length us, event | category | flops | bytes accessed | tf_op | source)
XLA Modules:
  0.0 216.9 jit_solution(5415309998487407140)
XLA Ops:
  0.0 216.0 %shard_map.28 = bf16[1,128,3072]{2,1,0:T(8,128)(2,1)S(1)} custom-call(bf16[1,128,3072]{2,1,0:T(8,128)(2,1)} %w_hbm.1, s32[1,8,256]{2,1,0:T(8,128)} %p_hbm.1), custom_call_target="tpu_custom_call" | custom-call | tf_op jit(solution)/shard_map/pallas_call | solution.py:426
  216.1 0.9 copy.4

commit v9 on v8

--- a/solution.py
+++ b/solution.py
@@ -27,7 +27,7 @@
 SEM, N_SEM = layout([
     ("near_raw", 1), ("in", 32), ("z_raw", 2), ("z_fwd", 32), ("perm", 10),
     ("z1", 8), ("z2", 8), ("z3", 4), ("z4", 4), ("x1", 8), ("x2", 4), ("y1", 4), ("y2", 4), ("y3", 4), ("out", 2), ("away", 4),
-    ("cost", 6 * 4), ("pair", 3 * 4), ("seen", 3),
+    ("cost", 6 * 4), ("pair", 3 * 4 + 2), ("seen", 3 + 2),
 ])
 
 
@@ -198,31 +198,68 @@
             out[rows, tile] = (
                 (own[rows, tile].astype(jnp.float32) + aligned) * (1.0 / math.sqrt(2.0))).astype(jnp.bfloat16)
 
-    def merge_with(fourth, perm_row, part, own, out, then=lambda q: None):
+    def merge_with(fourth, perm_row, part, own, out, then=None):
         mixing_of(fourth, perm_row)
-        for first_piece, count in ((0, 1), (1, 1), (2, 2)):
+        for first_piece, count in ((0, 1), (1, 1), (2, 2)) if then else ((0, 4),):
             mix_rows(0, pl.ds(first_piece * Q, count * Q), part, own, out)
-            for q in range(first_piece, first_piece + count):
+            for q in range(first_piece, first_piece + count) if then else ():
                 then(q)
 
-    def merge(level, perm_row, part, own, out, then=lambda q: None):
+    def merge(level, perm_row, part, own, out, then=None):
         merge_with(fourth_of(level), perm_row, part, own, out, then)
 
     def perm_of(at, r):
         return perms[at, 0, r:r + 1]
 
+    def split_seen(k):
+        both = mine_e[k] + near_e[k]
+        seen[0] = both.astype(jnp.bfloat16)
+        seen[1] = (both - seen[0].astype(jnp.float32)).astype(jnp.bfloat16)
+
+    def level_rows(k, rows, sem, part, own, out):
+        arrived(near_p.at[k, rows], sem)
+        cost = (mine_p[k, rows, pl.ds(0, N)] + near_p[k, rows, pl.ds(0, N)]) * (1.0 / math.sqrt(D))
+        squared = cost * cost
+        fourth = squared * squared
+        mixing = (onehot[rows] + fourth * (0.5 / (1.0 + jnp.sum(fourth, axis=1, keepdims=True)))).astype(jnp.bfloat16)
+        mix[1, rows] = mixing
+        through = (jnp.dot(mixing, seen[0], preferred_element_type=jnp.float32)
+                   + jnp.dot(mixing, seen[1], preferred_element_type=jnp.float32))
+        direct = mine_p[k, rows, pl.ds(N, N)] + near_p[k, rows, pl.ds(N, N)]
+        cost = (direct + through) * (1.0 / math.sqrt(2.0 * D))
+        squared = cost * cost
+        next_fourth[rows] = squared * squared
+        mix_rows(1, rows, part, own, out)
+
+    def product(rows_of, columns_of):
+        return lax.dot_general(
+            rows_of, columns_of, (((1,), (1,)), ((), ())), preferred_element_type=jnp.float32)
+
     cost_part(0, 0, raw.at[0, 1], raw.at[0, 0], 1)
     merge(0, perm_of(0, 0), raw.at[0, 1], raw.at[0, 0], first.at[0])
-    for s in range(2):
-        arrived(raw.at[1, s, pl.ds(pl.multiple_of(my_rows, H), H)], SEM["z_raw"] + s)
-    for q in range(8):
-        rows = pl.ds(pl.multiple_of(far_rows + q * step, step), step)
-        for e in range(2):
+    onehot[...] = onehot_of(perm_of(1, 0)).T
+    halves = [pl.ds(pl.multiple_of(my_rows, H), H), pl.ds(pl.multiple_of(far_rows, H), H)]
+    for e, rows in enumerate(halves):
+        if e == 0:
             for s in range(2):
-                arrived(raw.at[1, s, rows, piece(e)], SEM["z_fwd"] + q * 4 + e * 2 + s)
-    cost_part(1, 0, raw.at[1, 1], raw.at[1, 0], 1)
-    merge(1, perm_of(1, 0), raw.at[1, 1], raw.at[1, 0], first.at[1])
-    cost_part(2, 0, first.at[1], first.at[0], 1)
+                arrived(raw.at[1, s, rows], SEM["z_raw"] + s)
+        else:
+            for q in range(8):
+                at_rows = pl.ds(pl.multiple_of(far_rows + q * step, step), step)
+                for c in range(2):
+                    for s in range(2):
+                        arrived(raw.at[1, s, at_rows, piece(c)], SEM["z_fwd"] + q * 4 + c * 2 + s)
+        mine_e[3, rows] = product(raw[1, 1, rows], first[0])
+        send(mine_e.at[3, rows], near_e.at[3, rows], SEM["seen"] + 3 + e, near)
+        mine_p[3, rows, pl.ds(N, N)] = product(raw[1, 0, rows], first[0])
+    for e, rows in enumerate(halves):
+        mine_p[3, rows, pl.ds(0, N)] = product(raw[1, 0, rows], raw[1, 1])
+        send(mine_p.at[3, rows], near_p.at[3, rows], SEM["pair"] + 12 + e, near)
+    for e, rows in enumerate(halves):
+        arrived(near_e.at[3, rows], SEM["seen"] + 3 + e)
+    split_seen(3)
+    for e, rows in enumerate(halves):
+        level_rows(3, rows, SEM["pair"] + 12 + e, raw.at[1, 1], raw.at[1, 0], first.at[1])
 
     def quad(k, at, r, own, slots, wait_rings, order, wait_opposite, tmp):
         level = 3 + k
@@ -243,29 +280,14 @@
             send(mine_p.at[k, rows4(q)], near_p.at[k, rows4(q)], SEM["pair"] + 4 * k + q, near)
 
         def level_of(q):
-            rows = rows4(q)
-            arrived(near_p.at[k, rows], SEM["pair"] + 4 * k + q)
-            cost = (mine_p[k, rows, pl.ds(0, N)] + near_p[k, rows, pl.ds(0, N)]) * (1.0 / math.sqrt(D))
-            squared = cost * cost
-            fourth = squared * squared
-            mixing = (onehot[rows] + fourth * (0.5 / (1.0 + jnp.sum(fourth, axis=1, keepdims=True)))).astype(jnp.bfloat16)
-            mix[1, rows] = mixing
-            through = (jnp.dot(mixing, seen[0], preferred_element_type=jnp.float32)
-                       + jnp.dot(mixing, seen[1], preferred_element_type=jnp.float32))
-            direct = mine_p[k, rows, pl.ds(N, N)] + near_p[k, rows, pl.ds(N, N)]
-            cost = (direct + through) * (1.0 / math.sqrt(2.0 * D))
-            squared = cost * cost
-            next_fourth[rows] = squared * squared
-            mix_rows(1, rows, slots.at[2], slots.at[1], tmp.at[1])
+            level_rows(k, rows4(q), SEM["pair"] + 4 * k + q, slots.at[2], slots.at[1], tmp.at[1])
 
         for e, q in enumerate(order):
             wait_opposite(q)
             sums(q)
             if e == 0:
                 arrived(near_e.at[k], SEM["seen"] + k)
-                both = mine_e[k] + near_e[k]
-                seen[0] = both.astype(jnp.bfloat16)
-                seen[1] = (both - seen[0].astype(jnp.float32)).astype(jnp.bfloat16)
+                split_seen(k)
             else:
                 level_of(order[e - 1])
         level_of(order[-1])
@@ -282,7 +304,7 @@
     to_next, to_last = 2 * (1 - bit1((z + 1) % 8)), 2 * bit1((z + 7) % 8)
     from_last, from_next = 2 * (1 - bit1(z)), 2 * bit1(z)
 
-    merge(2, perm_of(0, 1), first.at[1], first.at[0], cur.at[0], send_z1)
+    merge_with(next_fourth[...], perm_of(0, 1), first.at[1], first.at[0], cur.at[0], send_z1)
     for q in range(4):
         arrived(relay.at[0, rows4(q)], SEM["z1"] + q)
         send(relay.at[0, rows4(q)], zq.at[to_next, rows4(q)], SEM["z2"] + q, z_next)
@@ -439,10 +461,10 @@
             pltpu.VMEM((2, H, F), jnp.bfloat16),
             pltpu.VMEM((6, N, N), jnp.float32),
             pltpu.VMEM((6, N, N), jnp.float32),
-            pltpu.VMEM((3, N, 2 * N), jnp.float32),
-            pltpu.VMEM((3, N, 2 * N), jnp.float32),
-            pltpu.VMEM((3, N, N), jnp.float32),
-            pltpu.VMEM((3, N, N), jnp.float32),
+            pltpu.VMEM((4, N, 2 * N), jnp.float32),
+            pltpu.VMEM((4, N, 2 * N), jnp.float32),
+            pltpu.VMEM((4, N, N), jnp.float32),
+            pltpu.VMEM((4, N, N), jnp.float32),
             pltpu.VMEM((2, N, N), jnp.bfloat16),
             pltpu.VMEM((N, N), jnp.float32),
             pltpu.VMEM((N, N), jnp.float32),

time: 217 us -> 218 us (level)
  no operation moved by 1% of the time
where the time goes in v9:
time: 218 us; the launch traced here: 216 us
  Pallas kernels  215 us (99%)
    pallas_call x1, Pallas kernels, local(): pl.pallas_call(kernel, out_shape=pltpu.VMEM((1, H, D), jnp.bfloat16), in_...  215 us

profile of v9, /device:TPU:57, one launch (start us, length us, event | category | flops | bytes accessed | tf_op | source)
XLA Modules:
  0.0 216.3 jit_solution(14499821021616855761)
XLA Ops:
  0.0 215.4 %shard_map.28 = bf16[1,128,3072]{2,1,0:T(8,128)(2,1)S(1)} custom-call(bf16[1,128,3072]{2,1,0:T(8,128)(2,1)} %w_hbm.1, s32[1,8,256]{2,1,0:T(8,128)} %p_hbm.1), custom_call_target="tpu_custom_call" | custom-call | tf_op jit(solution)/shard_map/pallas_call | solution.py:448
  215.4 0.9 copy.4

commit v10 on v8

--- a/solution.py
+++ b/solution.py
@@ -62,12 +62,12 @@
     y = (rep // 64) % 4
     inner = ((y + 1) // 2) % 2
     y_cross = (rep + 64 * (3 - 2 * y), h)
-    peers = [near, z_next, z_last, x_next, x_last, same[Y0], y_cross]
-    for c in range(2):
-        peers.append((core(rep, c), far))
-        peers.append((core(chip[Y1], c), far))
-        for b in (Z0, Z2, X1, Y1):
+    peers = [(core(rep, c), far) for c in range(2)]
+    for b in (Z2, X1, Y1, Z0):
+        for c in range(2):
             peers.append((core(chip[b], c), h))
+    peers += [(core(chip[Y1], c), far) for c in range(2)]
+    peers += [z_next, z_last, x_next, x_last, same[Y0], y_cross, near]
     barrier = pltpu.get_barrier_semaphore()
     for peer in peers:
         pl.semaphore_signal(barrier, inc=1, device_id=peer, device_id_type=MESH)
@@ -198,14 +198,14 @@
             out[rows, tile] = (
                 (own[rows, tile].astype(jnp.float32) + aligned) * (1.0 / math.sqrt(2.0))).astype(jnp.bfloat16)
 
-    def merge_with(fourth, perm_row, part, own, out, then=lambda q: None):
+    def merge_with(fourth, perm_row, part, own, out, then=None):
         mixing_of(fourth, perm_row)
-        for first_piece, count in ((0, 1), (1, 1), (2, 2)):
+        for first_piece, count in ((0, 1), (1, 1), (2, 2)) if then else ((0, 4),):
             mix_rows(0, pl.ds(first_piece * Q, count * Q), part, own, out)
-            for q in range(first_piece, first_piece + count):
+            for q in range(first_piece, first_piece + count) if then else ():
                 then(q)
 
-    def merge(level, perm_row, part, own, out, then=lambda q: None):
+    def merge(level, perm_row, part, own, out, then=None):
         merge_with(fourth_of(level), perm_row, part, own, out, then)
 
     def perm_of(at, r):

time: 217 us -> 217 us (level)
  no operation moved by 1% of the time
where the time goes in v10:
time: 217 us; the launch traced here: 216 us
  Pallas kernels  215 us (99%)
    pallas_call x1, Pallas kernels, local(): pl.pallas_call(kernel, out_shape=pltpu.VMEM((1, H, D), jnp.bfloat16), in_...  215 us

profile of v10, /device:TPU:57, one launch (start us, length us, event | category | flops | bytes accessed | tf_op | source)
XLA Modules:
  0.0 215.7 jit_solution(9431939177756283400)
XLA Ops:
  0.0 214.8 %shard_map.28 = bf16[1,128,3072]{2,1,0:T(8,128)(2,1)S(1)} custom-call(bf16[1,128,3072]{2,1,0:T(8,128)(2,1)} %w_hbm.1, s32[1,8,256]{2,1,0:T(8,128)} %p_hbm.1), custom_call_target="tpu_custom_call" | custom-call | tf_op jit(solution)/shard_map/pallas_call | solution.py:426
  214.8 0.9 copy.4
